TPU v7x, 32 devices: a whole 2x2x4 slice. The times are simulated.
32 devices in a mesh: pole: 2 (over y), prow: 4 (over z), pcol: 4 (over x, core).
Axes of the slice: x: 2, y: 2, z: 4, core: 2. Of those that a mesh axis runs over, the one named last changes fastest.
Arguments:
- ainv_anc: bfloat16 [2, 4096, 2048], P(None, ('pole', 'prow'), 'pcol'), parts along dimension 1, may hold values from -6 to 6
- panel: bfloat16 [2, 8, 1024, 256], P(None, 'pole', ('pcol', 'prow')), parts along dimension 1, may hold values from -6 to 6
- u_inv: bfloat16 [2, 8, 256, 256], P(None, 'pole'), parts along dimension 1, may hold values from -0.01171875 to 0.01171875
- k_inv: float32 [2, 8, 256, 256], P(None, ('pole', 'pcol')), parts along dimension 1, may hold values from -6 to 6
- structure: int32 [4, 4], replicated, may hold values from -1 to 7, as said below
Outputs:
- sel_inv: float32 [2, 4096, 1024], P(None, ('pole', 'prow'), 'pcol'), parts along dimension 1
- diag_inv: float32 [2, 8, 256, 256], P(None, ('pole', 'pcol')), parts along dimension 1
There are 2 independent parts, one for each index of `pole`. A program takes and returns all parts, laid end to end along the dimension named above; an argument that names none is the same for every part. Nothing has to cross between parts.
Inputs may be any that keep to these rules, and one draw needn't show every extreme that they name: `structure`: slots g * 1 to (g + 1) * 1 - 1 of row k hold distinct blocks of g * 2 to (g + 1) * 2 - 1 in rising order, followed by -1 for empty slots; each such group of each row holds at least one block, and for every g some row fills all 1 slots of group g.
All inputs are finite; a program needn't handle non-finite values.
Results may differ from a plain program's by a relative error of at most 0.005.
Values may be sent and summed in bfloat16 or wider, within the bound.
A program may use at most 128 MiB of HBM per device.

v0:
```python
import functools

import jax
import jax.numpy as jnp
from jax import lax
from jax.experimental import pallas as pl
from jax.experimental.pallas import tpu as pltpu
from jax.sharding import PartitionSpec as P

BF16 = jnp.bfloat16
F32 = jnp.float32


def cdot(left, right, dims=(((1,), (0,)), ((), ()))):
    def single(x, y):
        return lax.dot_general(x, y, dims, preferred_element_type=F32)

    real = single(left[0], right[0]) - single(left[1], right[1])
    imag = single(left[0], right[1]) + single(left[1], right[0])
    return real, imag


def remote(src, dst, send_sem, recv_sem, where):
    return pltpu.make_async_remote_copy(
        src_ref=src,
        dst_ref=dst,
        send_sem=send_sem,
        recv_sem=recv_sem,
        device_id=where,
        device_id_type=pl.DeviceIdType.MESH,
    )


def kernel(
    n_rows, n_cols, table, a_hbm, panel_hbm, u_hbm, k_hbm, sel_out, diag_out,
    av, pv, uv, pr, gather, pick_out, pick_in, acc, r_buf, sel_buf, kv, qsend_buf, qrecv_buf, tot,
    local_sem, p_send, p_recv, a_send, a_recv, g_send, g_recv, q_send, q_recv, t_send, t_recv,
):
    row = lax.axis_index("prow")
    col = lax.axis_index("pcol")
    width = u_hbm.shape[-1]
    part = panel_hbm.shape[2]
    pairs = n_cols // 2
    row_blocks = a_hbm.shape[1] // width
    col_blocks = a_hbm.shape[2] // width

    def peer(unit):
        return ((col // 2 + unit // 2) % pairs) * 2 + (col + unit) % 2

    copy_p = pltpu.make_async_copy(panel_hbm, pv, local_sem.at[0])
    copy_u = pltpu.make_async_copy(u_hbm.at[:, col], uv, local_sem.at[1])
    copy_a = pltpu.make_async_copy(a_hbm, av, local_sem.at[2])
    copy_k = pltpu.make_async_copy(k_hbm, kv, local_sem.at[3])
    copy_p.start()
    copy_u.start()

    barrier = pltpu.get_barrier_semaphore()
    for unit in range(1, n_cols):
        pl.semaphore_signal(barrier, inc=1, device_id={"pcol": peer(unit)}, device_id_type=pl.DeviceIdType.MESH)

    @pl.when(row > 0)
    def _():
        pl.semaphore_signal(barrier, inc=1, device_id={"prow": row - 1}, device_id_type=pl.DeviceIdType.MESH)

    @pl.when(row < n_rows - 1)
    def _():
        pl.semaphore_signal(barrier, inc=1, device_id={"prow": row + 1}, device_id_type=pl.DeviceIdType.MESH)

    ends = (row == 0).astype(jnp.int32) + (row == n_rows - 1).astype(jnp.int32)
    pl.semaphore_wait(barrier, n_cols + 1 - ends)

    def panel_copy(unit, source):
        return remote(
            pv.at[:, peer(unit)], pr.at[source], p_send.at[unit], p_recv.at[source], {"pcol": peer(unit)}
        )

    def pick_copy(unit, source):
        return remote(
            pick_out.at[unit], pick_in.at[source], a_send.at[unit], a_recv.at[source], {"pcol": peer(unit)}
        )

    def line_copy(unit, chunk, step, side):
        block = gather.at[unit, :, chunk]
        there = row + 1 if side == 0 else row - 1
        return remote(block, block, g_send.at[unit, side, step], g_recv.at[unit, chunk], {"prow": there})

    copy_p.wait()
    copy_a.start()
    for unit in range(1, n_cols):
        panel_copy(unit, col).start()
    copy_u.wait()

    def scale(unit):
        slot = peer(unit)
        if unit == 0:
            left = (pv[0, col], pv[1, col])
        else:
            panel_copy(unit, slot).wait_recv()
            left = (pr[slot, 0], pr[slot, 1])
        real, imag = cdot(left, (uv[0], uv[1]))
        live = (jnp.full((1, width), table[col, slot]) >= 0).astype(F32)
        gather[unit, 0, row] = (real * live).astype(BF16)
        gather[unit, 1, row] = (imag * live).astype(BF16)

        @pl.when(row < n_rows - 1)
        def _():
            line_copy(unit, row, 0, 0).start()

        @pl.when(row > 0)
        def _():
            line_copy(unit, row, 0, 1).start()

    def pick(unit):
        node = peer(unit)
        top = jnp.full((1, width), table[node, row]) - row * row_blocks
        side = jnp.full((1, width), table[node, col]) - col * col_blocks
        for plane in range(2):
            total = None
            for i in range(row_blocks):
                for j in range(col_blocks):
                    keep = ((top == i) & (side == j)).astype(F32).astype(BF16)
                    block = av[plane, i * width : (i + 1) * width, j * width : (j + 1) * width] * keep
                    total = block if total is None else total + block
            pick_out[unit, plane] = total

    scale(0)
    scale(1)
    copy_a.wait()
    copy_k.start()
    order = list(range(2, n_cols)) + [1]
    for unit in order:
        pick(unit)
        pick_copy(unit, col).start()
    pick(0)

    def forward(unit, step):
        below, above = row - step, row + step

        @pl.when(below >= 0)
        def _():
            line_copy(unit, below, step, 0).wait_recv()

            @pl.when(row < n_rows - 1)
            def _():
                line_copy(unit, below, step, 0).start()

        @pl.when(above <= n_rows - 1)
        def _():
            line_copy(unit, above, step, 1).wait_recv()

            @pl.when(row > 0)
            def _():
                line_copy(unit, above, step, 1).start()

    def multiply(unit):
        slot = peer(unit)
        if unit == 0:
            left = (pick_out[0, 0], pick_out[0, 1])
        else:
            pick_copy(unit, slot).wait_recv()
            left = (pick_in[slot, 0], pick_in[slot, 1])
        right = tuple(gather[unit, plane].reshape(width, width) for plane in range(2))
        real, imag = cdot(left, right)
        if unit == 0:
            acc[0] = real
            acc[1] = imag
        else:
            acc[0] += real
            acc[1] += imag

    early, late = (0, 1), range(2, n_cols)
    for unit in early:
        forward(unit, 1)
    for unit in late:
        scale(unit)
    for step in range(2, n_rows + 1):
        for unit in early:
            if step < n_rows:
                forward(unit, step)
        for unit in late:
            forward(unit, step - 1)
            if step == n_rows:
                multiply(unit)
        if step == n_rows - 1:
            for unit in early:
                multiply(unit)
    live = (jnp.full((1, width), table[col, row]) >= 0).astype(F32)
    unit_here = ((row // 2 - col // 2 + pairs) % pairs) * 2 + (row + col) % 2
    z = tuple(gather[unit_here, plane].reshape(width, width) for plane in range(2))
    r = (acc[0] * live, acc[1] * live)
    r_buf[0] = r[0]
    r_buf[1] = r[1]
    halves, pieces = 2, 2
    half_width = width // halves

    def diag_copy(half):
        columns = pl.ds(half * half_width, half_width)
        return pltpu.make_async_copy(
            kv.at[:, :, :, columns], diag_out.at[:, :, :, columns], local_sem.at[5 + half]
        )

    def band(piece):
        return pl.ds(piece * (part // pieces), part // pieces)

    def quad_copy(half, piece, step, source):
        there = (row + step) % n_rows
        return remote(
            qsend_buf.at[half, there, :, band(piece)], qrecv_buf.at[half, source, :, band(piece)],
            q_send.at[half, piece, step], q_recv.at[half, piece, source], {"prow": there},
        )

    def total_copy(half, piece, step, source):
        there = (row + step) % n_rows
        block = tot.at[half, source, :, band(piece)]
        return remote(block, block, t_send.at[half, piece, step], t_recv.at[half, piece, source], {"prow": there})

    low = (r[0].astype(BF16), r[1].astype(BF16))
    for half in range(halves):
        columns = slice(half * half_width, (half + 1) * half_width)
        quad = cdot(z, (low[0][:, columns], low[1][:, columns]), (((0,), (0,)), ((), ())))
        for plane in range(2):
            acc[plane, :, columns] = quad[plane]
            qsend_buf[half, :, plane] = quad[plane].reshape(n_rows, part, half_width).astype(BF16)
        for piece in range(pieces):
            for step in range(1, n_rows):
                quad_copy(half, piece, step, row).start()
    named = jnp.full((1, width), table[col, row]) - row * row_blocks
    for i in range(row_blocks):
        keep = -(named == i).astype(F32)
        for plane in range(2):
            sel_buf[plane, i * width : (i + 1) * width, :] = r_buf[plane] * keep
    copy_s = pltpu.make_async_copy(sel_buf, sel_out, local_sem.at[4])
    copy_s.start()
    copy_k.wait()
    rows_piece = part // pieces
    for half in range(halves):
        columns = slice(half * half_width, (half + 1) * half_width)
        for piece in range(pieces):
            mine = pl.ds(pl.multiple_of(row * part + piece * rows_piece, rows_piece), rows_piece)
            sums = [acc[0, mine, columns], acc[1, mine, columns]]
            for step in range(1, n_rows):
                source = (row + step) % n_rows
                quad_copy(half, piece, step, source).wait_recv()
                for plane in range(2):
                    sums[plane] = sums[plane] + qrecv_buf[half, source, plane, band(piece)].astype(F32)
            for plane in range(2):
                tot[half, row, plane, band(piece)] = sums[plane].astype(BF16)
            for step in range(1, n_rows):
                total_copy(half, piece, step, row).start()
    for half in range(halves):
        columns = slice(half * half_width, (half + 1) * half_width)
        for step in range(1, n_rows):
            for piece in range(pieces):
                total_copy(half, piece, step, (row + step) % n_rows).wait_recv()
        for plane in range(2):
            kv[plane, 0, :, columns] = (
                kv[plane, 0, :, columns] + tot[half, :, plane].reshape(width, half_width).astype(F32)
            )

        diag_copy(half).start()
    copy_s.wait()
    for half in range(halves):
        diag_copy(half).wait()
    for unit in range(1, n_cols):
        panel_copy(unit, col).wait_send()
        pick_copy(unit, col).wait_send()
    for unit in range(n_cols):
        for step in range(n_rows):
            below, above = row - step, row + step

            @pl.when((below >= 0) & (row < n_rows - 1))
            def _():
                line_copy(unit, below, step, 0).wait_send()

            @pl.when((above <= n_rows - 1) & (row > 0))
            def _():
                line_copy(unit, above, step, 1).wait_send()

    for step in range(1, n_rows):
        for half in range(halves):
            for piece in range(pieces):
                quad_copy(half, piece, step, row).wait_send()
                total_copy(half, piece, step, row).wait_send()


def place(cuts, sel_hbm, diag_hbm, sel_out, diag_out, sel_buf, diag_buf, in_sem, out_sem):
    rows = sel_hbm.shape[1] // cuts
    ins, outs = [], []
    for plane in range(2):
        for cut in range(cuts):
            at = (plane, pl.ds(cut * rows, rows))
            index = plane * (cuts + 1) + cut
            ins.append(pltpu.make_async_copy(sel_hbm.at[at], sel_buf.at[at], in_sem.at[index]))
            outs.append(pltpu.make_async_copy(sel_buf.at[at], sel_out.at[at], out_sem.at[index]))
        index = plane * (cuts + 1) + cuts
        ins.append(pltpu.make_async_copy(diag_hbm.at[plane], diag_buf.at[plane], in_sem.at[index]))
        outs.append(pltpu.make_async_copy(diag_buf.at[plane], diag_out.at[plane], out_sem.at[index]))
    for copy in ins:
        copy.start()
    for load, store in zip(ins, outs):
        load.wait()
        store.start()
    for copy in outs:
        copy.wait()


def compact(ainv_anc, panel, u_inv, k_inv, structure):
    n_rows, n_cols = lax.axis_size("prow"), lax.axis_size("pcol")
    width, part = u_inv.shape[-1], panel.shape[2]
    row_blocks = ainv_anc.shape[1] // width
    hbm = pl.BlockSpec(memory_space=pltpu.HBM)
    vmem = pl.BlockSpec(memory_space=pltpu.VMEM)
    dma = pltpu.SemaphoreType.DMA
    shapes = (
        jax.ShapeDtypeStruct((2, row_blocks * width, width), F32),
        jax.ShapeDtypeStruct(k_inv.shape, F32),
    )
    results = pl.pallas_call(
        functools.partial(kernel, n_rows, n_cols),
        out_shape=shapes,
        in_specs=[pl.BlockSpec(memory_space=pltpu.SMEM), hbm, hbm, hbm, hbm],
        out_specs=(hbm, hbm),
        scratch_shapes=[
            pltpu.VMEM(ainv_anc.shape, BF16),
            pltpu.VMEM(panel.shape, BF16),
            pltpu.VMEM((2, width, width), BF16),
            pltpu.VMEM((n_cols, 2, part, width), BF16),
            pltpu.VMEM((n_cols, 2, n_rows, part, width), BF16),
            pltpu.VMEM((n_cols, 2, width, width), BF16),
            pltpu.VMEM((n_cols, 2, width, width), BF16),
            pltpu.VMEM((2, width, width), F32),
            pltpu.VMEM((2, width, width), F32),
            pltpu.VMEM((2, row_blocks * width, width), F32),
            pltpu.VMEM(k_inv.shape, F32),
            pltpu.VMEM((2, n_rows, 2, part, width // 2), BF16),
            pltpu.VMEM((2, n_rows, 2, part, width // 2), BF16),
            pltpu.VMEM((2, n_rows, 2, part, width // 2), BF16),
            dma((7,)),
            dma((n_cols,)),
            dma((n_cols,)),
            dma((n_cols,)),
            dma((n_cols,)),
            dma((n_cols, 2, n_rows)),
            dma((n_cols, n_rows)),
            dma((2, 2, n_rows)),
            dma((2, 2, n_rows)),
            dma((2, 2, n_rows)),
            dma((2, 2, n_rows)),
        ],
        compiler_params=pltpu.CompilerParams(
            collective_id=0, has_side_effects=True
        ),
    )(structure, ainv_anc, panel, u_inv, k_inv)
    cuts = 2
    return pl.pallas_call(
        functools.partial(place, cuts),
        out_shape=shapes,
        in_specs=[hbm, hbm],
        out_specs=(hbm, hbm),
        scratch_shapes=[
            pltpu.VMEM(shapes[0].shape, F32),
            pltpu.VMEM(shapes[1].shape, F32),
            dma((2 * (cuts + 1),)),
            dma((2 * (cuts + 1),)),
        ],
    )(*results)


def complex_quad(z_part, s_part):
    highest = lax.Precision.HIGHEST

    def single(left, right):
        return jnp.einsum("kra,rkb->kab", left, right, precision=highest)

    real = single(z_part[0], s_part[0]) - single(z_part[1], s_part[1])
    imag = single(z_part[0], s_part[1]) + single(z_part[1], s_part[0])
    return jnp.stack([real, imag])


def local(ainv_anc, panel, u_inv, k_inv, structure):
    block_width = u_inv.shape[-1]
    cols = lax.axis_size("pcol")
    if (
        structure.shape[1] == cols
        and lax.axis_size("prow") == cols
        and ainv_anc.shape[1] == ainv_anc.shape[2]
        and u_inv.shape[1] == cols
        and cols % 2 == 0
    ):
        return compact(ainv_anc, panel, u_inv, k_inv, structure)
    total_k = u_inv.shape[1]
    own_k = k_inv.shape[1]
    n_cols = lax.axis_size("pcol")
    row_here = lax.axis_index("prow")
    col_here = lax.axis_index("pcol")
    row_blocks = ainv_anc.shape[1] // block_width
    group_blocks = ainv_anc.shape[2] // block_width
    group_slots = structure.shape[1] // n_cols
    rows_all = row_blocks * block_width
    col_struct = lax.dynamic_slice_in_dim(structure, col_here * group_slots, group_slots, 1)
    slot_live = col_struct >= 0
    slot_pos = col_struct - col_here * group_blocks
    first_block = row_here * row_blocks
    target = first_block + jnp.arange(row_blocks, dtype=jnp.int32)
    rows_in = lax.all_gather(panel, "prow", axis=2, tiled=True)

    def single(left, right):
        return jnp.einsum("knb,kbc->knc", left, right, preferred_element_type=jnp.float32)

    real = single(rows_in[0], u_inv[0]) - single(rows_in[1], u_inv[1])
    imag = single(rows_in[0], u_inv[1]) + single(rows_in[1], u_inv[0])
    placed = jnp.stack([real, imag]).astype(jnp.bfloat16)
    placed = placed.reshape(2, total_k, group_slots, block_width, block_width)
    placed = jnp.where(slot_live[None, :, :, None, None], placed, jnp.zeros((), jnp.bfloat16))
    block_ids = jnp.arange(group_blocks, dtype=jnp.int32)
    pick_table = (slot_pos[:, :, None] == block_ids[None, None, :]).astype(jnp.bfloat16)
    ainv_blocks = ainv_anc.reshape(2, rows_all, group_blocks, block_width)

    def one_node(items):
        table_k, rows_k = items
        picked = jnp.einsum(
            "sg,cigw->cisw", table_k, ainv_blocks, preferred_element_type=jnp.float32
        )
        picked = picked.astype(jnp.bfloat16).reshape(2, rows_all, group_slots * block_width)
        right = rows_k.reshape(2, group_slots * block_width, block_width)
        real = jnp.dot(picked[0], right[0], preferred_element_type=jnp.float32) - jnp.dot(
            picked[1], right[1], preferred_element_type=jnp.float32
        )
        imag = jnp.dot(picked[0], right[1], preferred_element_type=jnp.float32) + jnp.dot(
            picked[1], right[0], preferred_element_type=jnp.float32
        )
        return jnp.stack([real, imag])

    per_node = lax.map(one_node, (pick_table, jnp.moveaxis(placed, 1, 0)))
    partial_value = jnp.transpose(per_node, (1, 2, 0, 3))
    row_table = (col_struct[:, None, :] == target[None, :, None]).astype(jnp.bfloat16)
    z_rows = jnp.einsum("kts,ckswb->cktwb", row_table, placed, preferred_element_type=jnp.float32)
    z_rows = z_rows.astype(jnp.bfloat16).reshape(2, total_k, rows_all, block_width)
    summed = lax.psum_scatter(
        partial_value.reshape(2, rows_all, total_k * block_width),
        "pcol",
        scatter_dimension=2,
        tiled=True,
    )
    own_struct = lax.dynamic_slice_in_dim(structure, col_here * own_k, own_k, 0)
    member = jnp.any(own_struct[:, :, None] == target[None, None, :], axis=1)
    selected = -summed.reshape(2, row_blocks, block_width, own_k, block_width)
    selected = jnp.where(member.T[None, :, None, :, None], selected, 0.0)
    sel_inv = selected.reshape(2, rows_all, own_k * block_width)
    received = lax.all_to_all(z_rows, "pcol", split_axis=1, concat_axis=1, tiled=True)
    z_own = (
        received.astype(jnp.float32).reshape(2, n_cols, own_k, rows_all, block_width).sum(axis=1)
    )
    quad_term = complex_quad(z_own, selected.reshape(2, rows_all, own_k, block_width))
    total_sum = lax.psum(quad_term, "prow")
    diag_inv = k_inv - total_sum
    return (sel_inv, diag_inv)


def solution(mesh):
    placed = (
        P(None, ("pole", "prow"), "pcol"),
        P(None, "pole", ("pcol", "prow"), None),
        P(None, "pole", None, None),
        P(None, ("pole", "pcol"), None, None),
        P(),
    )
    return jax.shard_map(
        local,
        mesh=mesh,
        in_specs=placed,
        out_specs=(P(None, ("pole", "prow"), "pcol"), P(None, ("pole", "pcol"), None, None)),
        check_vma=False,
    )
```

profile of v0, /device:TPU:0, one launch (start us, length us, event | category | flops | bytes accessed | tf_op | source)
XLA Modules:
  0.0 42.8 jit_solution(9406063896892546508)
XLA Ops:
  0.6 40.0 %shard_map.68 = (f32[2,512,256]{2,1,0:T(8,128)}, f32[2,1,256,256]{3,2,1,0:T(8,128)}) custom-call(s32[4,4]{1,0:T(4,128)} %table.1, bf16[2,512,512]{2,1,0:T(8,128)(2,1)} %a_hbm.1, bf16[2,4,64,256]{3,2,1,0:T(8,128)(2,1)} %panel_hbm.1, bf16[2,4,256,256]{3,2,1,0:T(8,128)(2,1)} %u_hbm.1, f32[2,1,256,256]{3,2,1,0:T(8,128)} %k_hbm.1), custom_call_target="tpu_custom_call" | custom-call | tf_op jit(solution)/shard_map/pallas_call | solution.py:318
  40.6 2.2 %shard_map.69 = (f32[2,512,256]{2,1,0:T(8,128)}, f32[2,1,256,256]{3,2,1,0:T(8,128)}) custom-call(f32[2,512,256]{2,1,0:T(8,128)} %get-tuple-element.4.sel_hbm, f32[2,1,256,256]{3,2,1,0:T(8,128)} %get-tuple-element.5.diag_hbm), custom_call_target="tpu_custom_call" | custom-call | tf_op jit(solution)/shard_map/pallas_call | solution.py:355
where the time goes:
time: 43 us; the launch traced here: 42.8 us
  Pallas kernels  42.1 us (98%)
  between operations  0.64 us (1%)
    pallas_call x1, Pallas kernels, compact(): pl.pallas_call(functools.partial(kernel, n_rows, n_cols), out_shape=shape...  40 us
    pallas_call x1, Pallas kernels, compact(): pl.pallas_call(functools.partial(place, cuts), out_shape=shapes, in_specs...  2.19 us

commit v1 on v0

v1 whole, which is shorter than its diff:
```python
import functools

import jax
import jax.numpy as jnp
from jax import lax
from jax.experimental import pallas as pl
from jax.experimental.pallas import tpu as pltpu
from jax.sharding import PartitionSpec as P

BF16 = jnp.bfloat16
F32 = jnp.float32


def cdot(left, right, dims=(((1,), (0,)), ((), ()))):
    def single(x, y):
        return lax.dot_general(x, y, dims, preferred_element_type=F32)

    real = single(left[0], right[0]) - single(left[1], right[1])
    imag = single(left[0], right[1]) + single(left[1], right[0])
    return real, imag


def remote(src, dst, send_sem, recv_sem, where):
    return pltpu.make_async_remote_copy(
        src_ref=src,
        dst_ref=dst,
        send_sem=send_sem,
        recv_sem=recv_sem,
        device_id=where,
        device_id_type=pl.DeviceIdType.MESH,
    )


def kernel(
    n_rows, n_cols, bands, a_hbm, panel_hbm, u_hbm, k_hbm, table_hbm, sel_out, diag_out,
    table, av, pv, uv, pr, gather, pick_out, pick_in, acc, kv, q_out, q_in, tot, q_own,
    local_sem, p_send, p_recv, a_send, a_recv, g_send, g_recv, q_send, q_recv, t_send, t_recv,
):
    row = lax.axis_index("prow")
    col = lax.axis_index("pcol")
    width = u_hbm.shape[-1]
    pairs = n_cols // 2
    row_blocks = a_hbm.shape[1] // width
    col_blocks = a_hbm.shape[2] // width
    half_width = width // 2
    band_rows = width // bands
    mate = row + 1 - 2 * (row % 2)
    is_end = (row == 0) | (row == n_rows - 1)
    end = jnp.where(is_end, row, mate)
    inner = jnp.where(is_end, mate, row)
    over = n_rows - 1 - inner
    far = n_rows - 1 - end

    def peer(unit):
        return ((col // 2 + unit // 2) % pairs) * 2 + (col + unit) % 2

    copy_p = pltpu.make_async_copy(panel_hbm, pv, local_sem.at[0])
    copy_u = pltpu.make_async_copy(u_hbm.at[:, col], uv, local_sem.at[1])
    copy_t = pltpu.make_async_copy(table_hbm, table, local_sem.at[2])
    copy_a = pltpu.make_async_copy(a_hbm, av, local_sem.at[3])
    copy_k = pltpu.make_async_copy(k_hbm, kv, local_sem.at[4])
    copy_p.start()
    copy_u.start()
    copy_t.start()

    barrier = pltpu.get_barrier_semaphore()

    def greet(axis, there):
        pl.semaphore_signal(barrier, inc=1, device_id={axis: there}, device_id_type=pl.DeviceIdType.MESH)

    for unit in range(1, n_cols):
        greet("pcol", peer(unit))
    greet("prow", mate)
    greet("prow", jnp.where(is_end, over, far))

    @pl.when(jnp.logical_not(is_end))
    def _():
        greet("prow", over)

    pl.semaphore_wait(barrier, n_cols + 2 - is_end.astype(jnp.int32))

    def panel_copy(unit, source):
        return remote(
            pv.at[:, peer(unit)], pr.at[source], p_send.at[unit], p_recv.at[source], {"pcol": peer(unit)}
        )

    def pick_copy(unit, source):
        return remote(
            pick_out.at[unit], pick_in.at[source], a_send.at[unit], a_recv.at[source], {"pcol": peer(unit)}
        )

    def chunk_copy(unit, chunk, kind, there):
        block = gather.at[unit, :, chunk]
        return remote(block, block, g_send.at[kind], g_recv.at[unit, chunk], {"prow": there})

    def arrived(unit, chunk):
        chunk_copy(unit, chunk, 0, mate).wait_recv()

    copy_p.wait()
    copy_a.start()
    for unit in range(1, n_cols):
        panel_copy(unit, col).start()
    copy_k.start()
    copy_u.wait()
    copy_t.wait()

    def scale(unit):
        slot = peer(unit)
        if unit == 0:
            left = (pv[0, col], pv[1, col])
        else:
            panel_copy(unit, slot).wait_recv()
            left = (pr[slot, 0], pr[slot, 1])
        real, imag = cdot(left, (uv[0], uv[1]))
        live = (jnp.full((1, width), table[col, slot]) >= 0).astype(F32)
        gather[unit, 0, row] = (real * live).astype(BF16)
        gather[unit, 1, row] = (imag * live).astype(BF16)
        chunk_copy(unit, row, 0, over).start()
        chunk_copy(unit, row, 1, mate).start()

    def pick(unit):
        node = peer(unit)
        top = jnp.full((1, width), table[node, row]) - row * row_blocks
        side = jnp.full((1, width), table[node, col]) - col * col_blocks
        for plane in range(2):
            total = None
            for i in range(row_blocks):
                for j in range(col_blocks):
                    keep = ((top == i) & (side == j)).astype(F32).astype(BF16)
                    block = av[plane, i * width : (i + 1) * width, j * width : (j + 1) * width] * keep
                    total = block if total is None else total + block
            pick_out[unit, plane] = total

    scale(0)
    scale(1)
    copy_a.wait()
    for unit in list(range(2, n_cols)) + [1]:
        pick(unit)
        pick_copy(unit, col).start()
    pick(0)
    late = range(2, n_cols)

    def relay(unit, chunk, kind):
        arrived(unit, chunk)
        chunk_copy(unit, chunk, kind, end).start()

    @pl.when(is_end)
    def _():
        for unit in late:
            scale(unit)

    @pl.when(jnp.logical_not(is_end))
    def _():
        scale(2)
        relay(0, over, 2)
        scale(3)
        relay(1, over, 2)
        relay(0, far, 3)
        relay(1, far, 3)
        for unit in late:
            relay(unit, over, 2)
            relay(unit, far, 3)

    def multiply(unit):
        slot = peer(unit)

        @pl.when(is_end)
        def _():
            arrived(unit, over)
            arrived(unit, far)

        arrived(unit, mate)
        if unit == 0:
            left = (pick_out[0, 0], pick_out[0, 1])
        else:
            pick_copy(unit, slot).wait_recv()
            left = (pick_in[slot, 0], pick_in[slot, 1])
        right = tuple(gather[unit, plane].reshape(width, width) for plane in range(2))
        real, imag = cdot(left, right)
        if unit == 0:
            acc[0] = real
            acc[1] = imag
        else:
            acc[0] += real
            acc[1] += imag

    for unit in range(n_cols):
        multiply(unit)
    live = (jnp.full((1, width), table[col, row]) >= 0).astype(F32)
    unit_here = ((row // 2 - col // 2 + pairs) % pairs) * 2 + (row + col) % 2
    z = tuple(gather[unit_here, plane].reshape(width, width) for plane in range(2))
    r = (acc[0] * live, acc[1] * live)
    low = (r[0].astype(BF16), r[1].astype(BF16))
    named = jnp.full((1, width), table[col, row]) - row * row_blocks

    def owner(half):
        return n_rows // 2 - 1 + half

    def quad_copy(half, band, source):
        return remote(
            q_out.at[half, band], q_in.at[source, band], q_send.at[0], q_recv.at[source, band],
            {"prow": owner(half)},
        )

    def total_copy(half, band, kind, there):
        block = tot.at[half, band]
        return remote(block, block, t_send.at[kind], t_recv.at[half, band], {"prow": there})

    for half in range(2):
        columns = slice(half * half_width, (half + 1) * half_width)
        quad = cdot(z, (low[0][:, columns], low[1][:, columns]), (((0,), (0,)), ((), ())))
        for plane in range(2):
            for band in range(bands):
                block = quad[plane][band * band_rows : (band + 1) * band_rows]
                q_out[half, band, plane] = block.astype(BF16)

                @pl.when(row == owner(half))
                def _():
                    q_own[band, plane] = block

    for band in range(bands):
        for half in range(2):
            @pl.when(row != owner(half))
            def _():
                quad_copy(half, band, row).start()

    for i in range(row_blocks):
        keep = -(named == i).astype(F32)
        for plane in range(2):
            sel_out[plane, i * width : (i + 1) * width, :] = r[plane] * keep
    copy_k.wait()

    def finish(half, band):
        rows = slice(band * band_rows, (band + 1) * band_rows)
        columns = pl.ds(pl.multiple_of(half * half_width, half_width), half_width)
        for plane in range(2):
            diag_out[plane, 0, rows, columns] = kv[plane, 0, rows, columns] + tot[half, band, plane].astype(F32)

    mine = inner - (n_rows // 2 - 1)

    @pl.when(jnp.logical_not(is_end))
    def _():
        for band in range(bands):
            for source in (over, end, far):
                quad_copy(mine, band, source).wait_recv()
            for plane in range(2):
                total = q_own[band, plane]
                for source in (over, end, far):
                    total = total + q_in[source, band, plane].astype(F32)
                tot[mine, band, plane] = total.astype(BF16)
            total_copy(mine, band, 0, far).start()
            total_copy(mine, band, 1, end).start()
            total_copy(mine, band, 2, over).start()
        for band in range(bands):
            finish(mine, band)

    @pl.when(is_end)
    def _():
        for band in range(bands):
            total_copy(mine, band, 0, far).wait_recv()
            finish(mine, band)

    for band in range(bands):
        total_copy(1 - mine, band, 0, far).wait_recv()
        finish(1 - mine, band)

    for unit in range(1, n_cols):
        panel_copy(unit, col).wait_send()
        pick_copy(unit, col).wait_send()

    def drain(view, sem):
        remote(view, view, sem, sem, {"prow": mate}).wait_send()

    drain(gather.at[0], g_send.at[0])
    drain(gather.at[0], g_send.at[1])

    @pl.when(is_end)
    def _():
        drain(q_out, q_send.at[0])

    @pl.when(jnp.logical_not(is_end))
    def _():
        drain(gather.at[0], g_send.at[2])
        drain(gather.at[0], g_send.at[3])
        drain(q_out.at[0], q_send.at[0])
        for kind in range(3):
            drain(tot.at[0], t_send.at[kind])


def place(sel, diag, sel_out, diag_out, out_sem):
    copies = [
        pltpu.make_async_copy(sel, sel_out, out_sem.at[0]),
        pltpu.make_async_copy(diag, diag_out, out_sem.at[1]),
    ]
    for copy in copies:
        copy.start()
    for copy in copies:
        copy.wait()


def compact(ainv_anc, panel, u_inv, k_inv, structure):
    n_rows, n_cols = lax.axis_size("prow"), lax.axis_size("pcol")
    width, part = u_inv.shape[-1], panel.shape[2]
    row_blocks = ainv_anc.shape[1] // width
    bands = n_rows
    hbm = pl.BlockSpec(memory_space=pltpu.HBM)
    vmem = pl.BlockSpec(memory_space=pltpu.VMEM)
    dma = pltpu.SemaphoreType.DMA
    shapes = (
        jax.ShapeDtypeStruct((2, row_blocks * width, width), F32),
        jax.ShapeDtypeStruct(k_inv.shape, F32),
    )
    piece = (2, width // bands, width // 2)
    results = pl.pallas_call(
        functools.partial(kernel, n_rows, n_cols, bands),
        out_shape=tuple(pltpu.VMEM(s.shape, s.dtype) for s in shapes),
        in_specs=[hbm, hbm, hbm, hbm, hbm],
        out_specs=(vmem, vmem),
        scratch_shapes=[
            pltpu.SMEM(structure.shape, jnp.int32),
            pltpu.VMEM(ainv_anc.shape, BF16),
            pltpu.VMEM(panel.shape, BF16),
            pltpu.VMEM((2, width, width), BF16),
            pltpu.VMEM((n_cols, 2, part, width), BF16),
            pltpu.VMEM((n_cols, 2, n_rows, part, width), BF16),
            pltpu.VMEM((n_cols, 2, width, width), BF16),
            pltpu.VMEM((n_cols, 2, width, width), BF16),
            pltpu.VMEM((2, width, width), F32),
            pltpu.VMEM(k_inv.shape, F32),
            pltpu.VMEM((2, bands) + piece, BF16),
            pltpu.VMEM((n_rows, bands) + piece, BF16),
            pltpu.VMEM((2, bands) + piece, BF16),
            pltpu.VMEM((bands,) + piece, F32),
            dma((5,)),
            dma((n_cols,)),
            dma((n_cols,)),
            dma((n_cols,)),
            dma((n_cols,)),
            dma((4,)),
            dma((n_cols, n_rows)),
            dma((1,)),
            dma((n_rows, bands)),
            dma((3,)),
            dma((2, bands)),
        ],
        compiler_params=pltpu.CompilerParams(
            collective_id=0, has_side_effects=True
        ),
    )(ainv_anc, panel, u_inv, k_inv, structure)
    return pl.pallas_call(
        place,
        out_shape=shapes,
        in_specs=[vmem, vmem],
        out_specs=(hbm, hbm),
        scratch_shapes=[dma((2,))],
    )(*[pltpu.with_memory_space_constraint(x, pltpu.VMEM) for x in results])


def complex_quad(z_part, s_part):
    highest = lax.Precision.HIGHEST

    def single(left, right):
        return jnp.einsum("kra,rkb->kab", left, right, precision=highest)

    real = single(z_part[0], s_part[0]) - single(z_part[1], s_part[1])
    imag = single(z_part[0], s_part[1]) + single(z_part[1], s_part[0])
    return jnp.stack([real, imag])


def local(ainv_anc, panel, u_inv, k_inv, structure):
    block_width = u_inv.shape[-1]
    cols = lax.axis_size("pcol")
    if (
        structure.shape[1] == cols
        and lax.axis_size("prow") == cols
        and ainv_anc.shape[1] == ainv_anc.shape[2]
        and u_inv.shape[1] == cols
        and cols // 2 == 2
        and cols % 2 == 0
    ):
        return compact(ainv_anc, panel, u_inv, k_inv, structure)
    total_k = u_inv.shape[1]
    own_k = k_inv.shape[1]
    n_cols = lax.axis_size("pcol")
    row_here = lax.axis_index("prow")
    col_here = lax.axis_index("pcol")
    row_blocks = ainv_anc.shape[1] // block_width
    group_blocks = ainv_anc.shape[2] // block_width
    group_slots = structure.shape[1] // n_cols
    rows_all = row_blocks * block_width
    col_struct = lax.dynamic_slice_in_dim(structure, col_here * group_slots, group_slots, 1)
    slot_live = col_struct >= 0
    slot_pos = col_struct - col_here * group_blocks
    first_block = row_here * row_blocks
    target = first_block + jnp.arange(row_blocks, dtype=jnp.int32)
    rows_in = lax.all_gather(panel, "prow", axis=2, tiled=True)

    def single(left, right):
        return jnp.einsum("knb,kbc->knc", left, right, preferred_element_type=jnp.float32)

    real = single(rows_in[0], u_inv[0]) - single(rows_in[1], u_inv[1])
    imag = single(rows_in[0], u_inv[1]) + single(rows_in[1], u_inv[0])
    placed = jnp.stack([real, imag]).astype(jnp.bfloat16)
    placed = placed.reshape(2, total_k, group_slots, block_width, block_width)
    placed = jnp.where(slot_live[None, :, :, None, None], placed, jnp.zeros((), jnp.bfloat16))
    block_ids = jnp.arange(group_blocks, dtype=jnp.int32)
    pick_table = (slot_pos[:, :, None] == block_ids[None, None, :]).astype(jnp.bfloat16)
    ainv_blocks = ainv_anc.reshape(2, rows_all, group_blocks, block_width)

    def one_node(items):
        table_k, rows_k = items
        picked = jnp.einsum(
            "sg,cigw->cisw", table_k, ainv_blocks, preferred_element_type=jnp.float32
        )
        picked = picked.astype(jnp.bfloat16).reshape(2, rows_all, group_slots * block_width)
        right = rows_k.reshape(2, group_slots * block_width, block_width)
        real = jnp.dot(picked[0], right[0], preferred_element_type=jnp.float32) - jnp.dot(
            picked[1], right[1], preferred_element_type=jnp.float32
        )
        imag = jnp.dot(picked[0], right[1], preferred_element_type=jnp.float32) + jnp.dot(
            picked[1], right[0], preferred_element_type=jnp.float32
        )
        return jnp.stack([real, imag])

    per_node = lax.map(one_node, (pick_table, jnp.moveaxis(placed, 1, 0)))
    partial_value = jnp.transpose(per_node, (1, 2, 0, 3))
    row_table = (col_struct[:, None, :] == target[None, :, None]).astype(jnp.bfloat16)
    z_rows = jnp.einsum("kts,ckswb->cktwb", row_table, placed, preferred_element_type=jnp.float32)
    z_rows = z_rows.astype(jnp.bfloat16).reshape(2, total_k, rows_all, block_width)
    summed = lax.psum_scatter(
        partial_value.reshape(2, rows_all, total_k * block_width),
        "pcol",
        scatter_dimension=2,
        tiled=True,
    )
    own_struct = lax.dynamic_slice_in_dim(structure, col_here * own_k, own_k, 0)
    member = jnp.any(own_struct[:, :, None] == target[None, None, :], axis=1)
    selected = -summed.reshape(2, row_blocks, block_width, own_k, block_width)
    selected = jnp.where(member.T[None, :, None, :, None], selected, 0.0)
    sel_inv = selected.reshape(2, rows_all, own_k * block_width)
    received = lax.all_to_all(z_rows, "pcol", split_axis=1, concat_axis=1, tiled=True)
    z_own = (
        received.astype(jnp.float32).reshape(2, n_cols, own_k, rows_all, block_width).sum(axis=1)
    )
    quad_term = complex_quad(z_own, selected.reshape(2, rows_all, own_k, block_width))
    total_sum = lax.psum(quad_term, "prow")
    diag_inv = k_inv - total_sum
    return (sel_inv, diag_inv)


def solution(mesh):
    placed = (
        P(None, ("pole", "prow"), "pcol"),
        P(None, "pole", ("pcol", "prow"), None),
        P(None, "pole", None, None),
        P(None, ("pole", "pcol"), None, None),
        P(),
    )
    return jax.shard_map(
        local,
        mesh=mesh,
        in_specs=placed,
        out_specs=(P(None, ("pole", "prow"), "pcol"), P(None, ("pole", "pcol"), None, None)),
        check_vma=False,
    )
```

time: 43 us -> 39.2 us (0.912)
  Pallas kernels: 42.1 us -> 38.4 us
    pallas_call x2, Pallas kernels: 42.1 us -> 38.4 us  [the longest x1 37.2 us: compact(): pl.pallas_call(functools.partial(kernel, n_rows, n_cols, bands), out_shap...]
where the time goes in v1:
time: 39.2 us; the launch traced here: 39 us
  Pallas kernels  38.4 us (98%)
  between operations  0.64 us (2%)
    pallas_call x1, Pallas kernels, compact(): pl.pallas_call(functools.partial(kernel, n_rows, n_cols, bands), out_shap...  37.2 us
    pallas_call x1, Pallas kernels, compact(): pl.pallas_call(place, out_shape=shapes, in_specs=[vmem, vmem], out_specs=...  1.16 us

profile of v1, /device:TPU:0, one launch (start us, length us, event | category | flops | bytes accessed | tf_op | source)
XLA Modules:
  0.0 39.0 jit_solution(7181823670670360955)
XLA Ops:
  0.6 37.2 %shard_map.68 = (f32[2,512,256]{2,1,0:T(8,128)S(1)}, f32[2,1,256,256]{3,2,1,0:T(8,128)S(1)}) custom-call(bf16[2,512,512]{2,1,0:T(8,128)(2,1)} %a_hbm.1, bf16[2,4,64,256]{3,2,1,0:T(8,128)(2,1)} %panel_hbm.1, bf16[2,4,256,256]{3,2,1,0:T(8,128)(2,1)} %u_hbm.1, f32[2,1,256,256]{3,2,1,0:T(8,128)} %k_hbm.1, s32[4,4]{1,0:T(4,128)} %table_hbm.1), custom_call_target="tpu_custom_call" | custom-call | tf_op jit(solution)/shard_map/pallas_call | solution.py:314
  37.9 1.2 %shard_map.69 = (f32[2,512,256]{2,1,0:T(8,128)}, f32[2,1,256,256]{3,2,1,0:T(8,128)}) custom-call(f32[2,512,256]{2,1,0:T(8,128)S(1)} %get-tuple-element.4.sel, f32[2,1,256,256]{3,2,1,0:T(8,128)S(1)} %get-tuple-element.5.diag), custom_call_target="tpu_custom_call" | custom-call | tf_op jit(solution)/shard_map/pallas_call | solution.py:350

commit v2 on v1

--- a/solution.py
+++ b/solution.py
@@ -9,6 +9,7 @@
 
 BF16 = jnp.bfloat16
 F32 = jnp.float32
+scope = jax.named_scope
 
 
 def cdot(left, right, dims=(((1,), (0,)), ((), ()))):
@@ -32,8 +33,8 @@
 
 
 def kernel(
-    n_rows, n_cols, bands, a_hbm, panel_hbm, u_hbm, k_hbm, table_hbm, sel_out, diag_out,
-    table, av, pv, uv, pr, gather, pick_out, pick_in, acc, kv, q_out, q_in, tot, q_own,
+    n_rows, n_cols, a_hbm, panel_hbm, u_hbm, k_hbm, table_hbm, sel_out, diag_out,
+    table, av, pv, uv, pr, gather, pick_out, picks, acc, kv, q_own, q_out, q_in, tot,
     local_sem, p_send, p_recv, a_send, a_recv, g_send, g_recv, q_send, q_recv, t_send, t_recv,
 ):
     row = lax.axis_index("prow")
@@ -42,10 +43,13 @@
     pairs = n_cols // 2
     row_blocks = a_hbm.shape[1] // width
     col_blocks = a_hbm.shape[2] // width
-    half_width = width // 2
-    band_rows = width // bands
+    lanes = width // 2
+    share = q_in.shape[2]
+    band_rows = q_in.shape[3]
+    bands = q_out.shape[1]
     mate = row + 1 - 2 * (row % 2)
     is_end = (row == 0) | (row == n_rows - 1)
+    is_inner = jnp.logical_not(is_end)
     end = jnp.where(is_end, row, mate)
     inner = jnp.where(is_end, mate, row)
     over = n_rows - 1 - inner
@@ -53,6 +57,9 @@
 
     def peer(unit):
         return ((col // 2 + unit // 2) % pairs) * 2 + (col + unit) % 2
+
+    def unit_of(slot):
+        return ((slot // 2 - col // 2 + pairs) % pairs) * 2 + (slot + col) % 2
 
     copy_p = pltpu.make_async_copy(panel_hbm, pv, local_sem.at[0])
     copy_u = pltpu.make_async_copy(u_hbm.at[:, col], uv, local_sem.at[1])
@@ -73,11 +80,12 @@
     greet("prow", mate)
     greet("prow", jnp.where(is_end, over, far))
 
-    @pl.when(jnp.logical_not(is_end))
+    @pl.when(is_inner)
     def _():
         greet("prow", over)
 
-    pl.semaphore_wait(barrier, n_cols + 2 - is_end.astype(jnp.int32))
+    with scope("barrier"):
+        pl.semaphore_wait(barrier, n_cols + 2 - is_end.astype(jnp.int32))
 
     def panel_copy(unit, source):
         return remote(
@@ -86,23 +94,25 @@
 
     def pick_copy(unit, source):
         return remote(
-            pick_out.at[unit], pick_in.at[source], a_send.at[unit], a_recv.at[source], {"pcol": peer(unit)}
+            pick_out.at[unit - 1], picks.at[source], a_send.at[unit], a_recv.at[source], {"pcol": peer(unit)}
         )
 
-    def chunk_copy(unit, chunk, kind, there):
-        block = gather.at[unit, :, chunk]
-        return remote(block, block, g_send.at[kind], g_recv.at[unit, chunk], {"prow": there})
-
-    def arrived(unit, chunk):
-        chunk_copy(unit, chunk, 0, mate).wait_recv()
-
-    copy_p.wait()
+    def chunk_copy(half, unit, chunk, kind, there):
+        block = gather.at[half, unit, chunk]
+        return remote(block, block, g_send.at[kind], g_recv.at[half, unit, chunk], {"prow": there})
+
+    def arrived(half, unit, chunk):
+        chunk_copy(half, unit, chunk, 0, mate).wait_recv()
+
+    with scope("copy_p"):
+        copy_p.wait()
     copy_a.start()
     for unit in range(1, n_cols):
         panel_copy(unit, col).start()
     copy_k.start()
-    copy_u.wait()
-    copy_t.wait()
+    with scope("copy_u"):
+        copy_u.wait()
+        copy_t.wait()
 
     def scale(unit):
         slot = peer(unit)
@@ -111,12 +121,16 @@
         else:
             panel_copy(unit, slot).wait_recv()
             left = (pr[slot, 0], pr[slot, 1])
-        real, imag = cdot(left, (uv[0], uv[1]))
-        live = (jnp.full((1, width), table[col, slot]) >= 0).astype(F32)
-        gather[unit, 0, row] = (real * live).astype(BF16)
-        gather[unit, 1, row] = (imag * live).astype(BF16)
-        chunk_copy(unit, row, 0, over).start()
-        chunk_copy(unit, row, 1, mate).start()
+        value = cdot(left, (uv[0], uv[1]))
+        live = (jnp.full((1, lanes), table[col, slot]) >= 0).astype(F32)
+        for half in range(2):
+            for plane in range(2):
+                block = value[plane][:, half * lanes : (half + 1) * lanes]
+                gather[half, unit, row, :, plane * lanes : (plane + 1) * lanes] = (block * live).astype(BF16)
+
+    def spread(half, unit):
+        chunk_copy(half, unit, row, 0, over).start()
+        chunk_copy(half, unit, row, 1, mate).start()
 
     def pick(unit):
         node = peer(unit)
@@ -129,140 +143,199 @@
                     keep = ((top == i) & (side == j)).astype(F32).astype(BF16)
                     block = av[plane, i * width : (i + 1) * width, j * width : (j + 1) * width] * keep
                     total = block if total is None else total + block
-            pick_out[unit, plane] = total
-
-    scale(0)
-    scale(1)
-    copy_a.wait()
+            if unit == 0:
+                picks[col, plane] = total
+            else:
+                pick_out[unit - 1, plane] = total
+
+    for unit in range(2):
+        with scope(f"scale{unit}"):
+            scale(unit)
+        for half in range(2):
+            spread(half, unit)
+    with scope("copy_a"):
+        copy_a.wait()
     for unit in list(range(2, n_cols)) + [1]:
-        pick(unit)
+        with scope(f"pick{unit}"):
+            pick(unit)
         pick_copy(unit, col).start()
     pick(0)
     late = range(2, n_cols)
 
-    def relay(unit, chunk, kind):
-        arrived(unit, chunk)
-        chunk_copy(unit, chunk, kind, end).start()
+    def relay(half, unit, chunk, kind):
+        arrived(half, unit, chunk)
+        chunk_copy(half, unit, chunk, kind, end).start()
 
     @pl.when(is_end)
     def _():
         for unit in late:
-            scale(unit)
-
-    @pl.when(jnp.logical_not(is_end))
+            with scope(f"scale{unit}"):
+                scale(unit)
+            spread(0, unit)
+        for unit in late:
+            spread(1, unit)
+
+    @pl.when(is_inner)
     def _():
-        scale(2)
-        relay(0, over, 2)
-        scale(3)
-        relay(1, over, 2)
-        relay(0, far, 3)
-        relay(1, far, 3)
+        with scope("scale2"):
+            scale(2)
+        spread(0, 2)
+        with scope("relay_0o"):
+            relay(0, 0, over, 2)
+        with scope("relay_1o"):
+            relay(0, 1, over, 2)
+        with scope("scale3"):
+            scale(3)
+        spread(0, 3)
+        with scope("relay_01f"):
+            relay(0, 0, far, 3)
+            relay(0, 1, far, 3)
         for unit in late:
-            relay(unit, over, 2)
-            relay(unit, far, 3)
-
-    def multiply(unit):
-        slot = peer(unit)
-
+            spread(1, unit)
+        for unit in late:
+            with scope(f"relay_{unit}o"):
+                relay(0, unit, over, 2)
+            with scope(f"relay_{unit}f"):
+                relay(0, unit, far, 3)
+        for i in range(n_cols):
+            unit = (unit_of(end) + i) % n_cols
+            with scope(f"relay_h1_{i}o"):
+                relay(1, unit, over, 2)
+            with scope(f"relay_h1_{i}f"):
+                relay(1, unit, far, 3)
+
+    def ready(half, unit):
         @pl.when(is_end)
         def _():
-            arrived(unit, over)
-            arrived(unit, far)
-
-        arrived(unit, mate)
-        if unit == 0:
-            left = (pick_out[0, 0], pick_out[0, 1])
-        else:
-            pick_copy(unit, slot).wait_recv()
-            left = (pick_in[slot, 0], pick_in[slot, 1])
-        right = tuple(gather[unit, plane].reshape(width, width) for plane in range(2))
-        real, imag = cdot(left, right)
-        if unit == 0:
-            acc[0] = real
-            acc[1] = imag
-        else:
-            acc[0] += real
-            acc[1] += imag
+            arrived(half, unit, over)
+            arrived(half, unit, far)
+
+        arrived(half, unit, mate)
+
+    def multiply(half, unit, first):
+        right = gather[half, unit].reshape(width, width)
+        slot = peer(unit)
+        for plane in range(2):
+            value = jnp.dot(picks[slot, plane], right, preferred_element_type=F32)
+            if first:
+                acc[plane] = value
+            else:
+                acc[plane] += value
+
+    home = unit_of(row)
+    live = (jnp.full((1, width), table[col, row]) >= 0).astype(F32)
+    named = jnp.full((1, lanes), table[col, row]) - row * row_blocks
+
+    def owner(band):
+        return n_rows // 2 - 1 + band // share
+
+    def quad_copy(half, there, part, source):
+        band = (there - (n_rows // 2 - 1)) * share + part
+        return remote(
+            q_out.at[half, band], q_in.at[source, half, part], q_send.at[0], q_recv.at[source, half, part],
+            {"prow": there},
+        )
+
+    def quad(half):
+        real = acc[0, :, :lanes] - acc[1, :, lanes:]
+        imag = acc[0, :, lanes:] + acc[1, :, :lanes]
+        value = jnp.concatenate([real, imag], axis=1) * live
+        low = value.astype(BF16)
+        for top in range(2):
+            z = gather[top, home].reshape(width, width)
+            product = lax.dot_general(z, low, (((0,), (0,)), ((), ())), preferred_element_type=F32)
+            real = product[:lanes, :lanes] - product[lanes:, lanes:]
+            imag = product[:lanes, lanes:] + product[lanes:, :lanes]
+            whole = jnp.concatenate([real, imag], axis=1)
+            for i in range(bands // 2):
+                block = whole[i * band_rows : (i + 1) * band_rows]
+                band = top * (bands // 2) + i
+                q_out[half, band] = block.astype(BF16)
+
+                @pl.when(row == owner(band))
+                def _():
+                    q_own[half, band % share] = block
+
+        for part in range(share):
+            quad_copy(half, over, part, row).start()
+
+        @pl.when(is_end)
+        def _():
+            for part in range(share):
+                quad_copy(half, mate, part, row).start()
+
+        columns = slice(half * lanes, (half + 1) * lanes)
+        for i in range(row_blocks):
+            keep = -(named == i).astype(F32)
+            for plane in range(2):
+                block = value[:, plane * lanes : (plane + 1) * lanes]
+                sel_out[plane, i * width : (i + 1) * width, columns] = block * keep
 
     for unit in range(n_cols):
-        multiply(unit)
-    live = (jnp.full((1, width), table[col, row]) >= 0).astype(F32)
-    unit_here = ((row // 2 - col // 2 + pairs) % pairs) * 2 + (row + col) % 2
-    z = tuple(gather[unit_here, plane].reshape(width, width) for plane in range(2))
-    r = (acc[0] * live, acc[1] * live)
-    low = (r[0].astype(BF16), r[1].astype(BF16))
-    named = jnp.full((1, width), table[col, row]) - row * row_blocks
-
-    def owner(half):
-        return n_rows // 2 - 1 + half
-
-    def quad_copy(half, band, source):
-        return remote(
-            q_out.at[half, band], q_in.at[source, band], q_send.at[0], q_recv.at[source, band],
-            {"prow": owner(half)},
-        )
+        with scope(f"ready_h0_{unit}"):
+            ready(0, unit)
+        with scope(f"wpick_{unit}"):
+            if unit > 0:
+                pick_copy(unit, peer(unit)).wait_recv()
+        multiply(0, unit, unit == 0)
+    with scope("ready_home"):
+        ready(1, home)
+    with scope("quad0"):
+        quad(0)
+    for i in range(n_cols):
+        unit = (home + i) % n_cols
+        if i > 0:
+            with scope(f"ready_h1_{i}"):
+                ready(1, unit)
+        multiply(1, unit, i == 0)
+    with scope("quad1"):
+        quad(1)
+    copy_k.wait()
 
     def total_copy(half, band, kind, there):
         block = tot.at[half, band]
         return remote(block, block, t_send.at[kind], t_recv.at[half, band], {"prow": there})
 
+    def finish(half, band):
+        rows = pl.ds(pl.multiple_of(band * band_rows, band_rows), band_rows)
+        columns = slice(half * lanes, (half + 1) * lanes)
+        for plane in range(2):
+            block = tot[half, band, :, plane * lanes : (plane + 1) * lanes].astype(F32)
+            diag_out[plane, 0, rows, columns] = kv[plane, 0, rows, columns] + block
+
+    near_band = (inner - (n_rows // 2 - 1)) * share
+    over_band = (over - (n_rows // 2 - 1)) * share
+
+    @pl.when(is_inner)
+    def _():
+        for half in range(2):
+            for part in range(share):
+                with scope(f"wq{half}_{part}"):
+                    for source in (over, end, far):
+                        quad_copy(half, row, part, source).wait_recv()
+                total = q_own[half, part]
+                for source in (over, end, far):
+                    total = total + q_in[source, half, part].astype(F32)
+                tot[half, near_band + part] = total.astype(BF16)
+                total_copy(half, near_band + part, 0, far).start()
+                total_copy(half, near_band + part, 1, end).start()
+                total_copy(half, near_band + part, 2, over).start()
+        for half in range(2):
+            for part in range(share):
+                finish(half, near_band + part)
+
     for half in range(2):
-        columns = slice(half * half_width, (half + 1) * half_width)
-        quad = cdot(z, (low[0][:, columns], low[1][:, columns]), (((0,), (0,)), ((), ())))
-        for plane in range(2):
-            for band in range(bands):
-                block = quad[plane][band * band_rows : (band + 1) * band_rows]
-                q_out[half, band, plane] = block.astype(BF16)
-
-                @pl.when(row == owner(half))
-                def _():
-                    q_own[band, plane] = block
-
-    for band in range(bands):
-        for half in range(2):
-            @pl.when(row != owner(half))
-            def _():
-                quad_copy(half, band, row).start()
-
-    for i in range(row_blocks):
-        keep = -(named == i).astype(F32)
-        for plane in range(2):
-            sel_out[plane, i * width : (i + 1) * width, :] = r[plane] * keep
-    copy_k.wait()
-
-    def finish(half, band):
-        rows = slice(band * band_rows, (band + 1) * band_rows)
-        columns = pl.ds(pl.multiple_of(half * half_width, half_width), half_width)
-        for plane in range(2):
-            diag_out[plane, 0, rows, columns] = kv[plane, 0, rows, columns] + tot[half, band, plane].astype(F32)
-
-    mine = inner - (n_rows // 2 - 1)
-
-    @pl.when(jnp.logical_not(is_end))
-    def _():
-        for band in range(bands):
-            for source in (over, end, far):
-                quad_copy(mine, band, source).wait_recv()
-            for plane in range(2):
-                total = q_own[band, plane]
-                for source in (over, end, far):
-                    total = total + q_in[source, band, plane].astype(F32)
-                tot[mine, band, plane] = total.astype(BF16)
-            total_copy(mine, band, 0, far).start()
-            total_copy(mine, band, 1, end).start()
-            total_copy(mine, band, 2, over).start()
-        for band in range(bands):
-            finish(mine, band)
-
-    @pl.when(is_end)
-    def _():
-        for band in range(bands):
-            total_copy(mine, band, 0, far).wait_recv()
-            finish(mine, band)
-
-    for band in range(bands):
-        total_copy(1 - mine, band, 0, far).wait_recv()
-        finish(1 - mine, band)
+        @pl.when(is_end)
+        def _():
+            for part in range(share):
+                with scope(f"wt_near{half}_{part}"):
+                    total_copy(half, near_band + part, 0, mate).wait_recv()
+                finish(half, near_band + part)
+
+        for part in range(share):
+            with scope(f"wt_over{half}_{part}"):
+                total_copy(half, over_band + part, 0, mate).wait_recv()
+            finish(half, over_band + part)
 
     for unit in range(1, n_cols):
         panel_copy(unit, col).wait_send()
@@ -271,17 +344,17 @@
     def drain(view, sem):
         remote(view, view, sem, sem, {"prow": mate}).wait_send()
 
-    drain(gather.at[0], g_send.at[0])
-    drain(gather.at[0], g_send.at[1])
+    drain(gather.at[0, 0:2], g_send.at[0])
+    drain(gather.at[0, 0:2], g_send.at[1])
 
     @pl.when(is_end)
     def _():
         drain(q_out, q_send.at[0])
 
-    @pl.when(jnp.logical_not(is_end))
+    @pl.when(is_inner)
     def _():
-        drain(gather.at[0], g_send.at[2])
-        drain(gather.at[0], g_send.at[3])
+        drain(gather.at[0, 0:2], g_send.at[2])
+        drain(gather.at[0, 0:2], g_send.at[3])
         drain(q_out.at[0], q_send.at[0])
         for kind in range(3):
             drain(tot.at[0], t_send.at[kind])
@@ -303,6 +376,7 @@
     width, part = u_inv.shape[-1], panel.shape[2]
     row_blocks = ainv_anc.shape[1] // width
     bands = n_rows
+    share = bands // 2
     hbm = pl.BlockSpec(memory_space=pltpu.HBM)
     vmem = pl.BlockSpec(memory_space=pltpu.VMEM)
     dma = pltpu.SemaphoreType.DMA
@@ -310,9 +384,9 @@
         jax.ShapeDtypeStruct((2, row_blocks * width, width), F32),
         jax.ShapeDtypeStruct(k_inv.shape, F32),
     )
-    piece = (2, width // bands, width // 2)
+    piece = (width // bands, width)
     results = pl.pallas_call(
-        functools.partial(kernel, n_rows, n_cols, bands),
+        functools.partial(kernel, n_rows, n_cols),
         out_shape=tuple(pltpu.VMEM(s.shape, s.dtype) for s in shapes),
         in_specs=[hbm, hbm, hbm, hbm, hbm],
         out_specs=(vmem, vmem),
@@ -322,24 +396,24 @@
             pltpu.VMEM(panel.shape, BF16),
             pltpu.VMEM((2, width, width), BF16),
             pltpu.VMEM((n_cols, 2, part, width), BF16),
-            pltpu.VMEM((n_cols, 2, n_rows, part, width), BF16),
-            pltpu.VMEM((n_cols, 2, width, width), BF16),
+            pltpu.VMEM((2, n_cols, n_rows, part, width), BF16),
+            pltpu.VMEM((n_cols - 1, 2, width, width), BF16),
             pltpu.VMEM((n_cols, 2, width, width), BF16),
             pltpu.VMEM((2, width, width), F32),
             pltpu.VMEM(k_inv.shape, F32),
+            pltpu.VMEM((2, share) + piece, F32),
             pltpu.VMEM((2, bands) + piece, BF16),
-            pltpu.VMEM((n_rows, bands) + piece, BF16),
+            pltpu.VMEM((n_rows, 2, share) + piece, BF16),
             pltpu.VMEM((2, bands) + piece, BF16),
-            pltpu.VMEM((bands,) + piece, F32),
             dma((5,)),
             dma((n_cols,)),
             dma((n_cols,)),
             dma((n_cols,)),
             dma((n_cols,)),
             dma((4,)),
-            dma((n_cols, n_rows)),
+            dma((2, n_cols, n_rows)),
             dma((1,)),
-            dma((n_rows, bands)),
+            dma((n_rows, 2, share)),
             dma((3,)),
             dma((2, bands)),
         ],

time: 39.2 us -> 36.8 us (0.939)
  Pallas kernels: 38.4 us -> 36 us
    pallas_call x1, Pallas kernels: 37.2 us -> 34.8 us  [compact(): pl.pallas_call(functools.partial(kernel, n_rows, n_cols), out_shape=tuple...]
where the time goes in v2:
time: 36.8 us; the launch traced here: 36.6 us
  Pallas kernels  36 us (98%)
  between operations  0.64 us (2%)
    pallas_call x1, Pallas kernels, compact(): pl.pallas_call(functools.partial(kernel, n_rows, n_cols), out_shape=tuple...  34.8 us
    pallas_call x1, Pallas kernels, compact(): pl.pallas_call(place, out_shape=shapes, in_specs=[vmem, vmem], out_specs=...  1.16 us

profile of v2, /device:TPU:0, one launch (start us, length us, event | category | flops | bytes accessed | tf_op | source)
XLA Modules:
  0.0 36.6 jit_solution(1319316239800198372)
XLA Ops:
  0.6 34.8 %shard_map.68 = (f32[2,512,256]{2,1,0:T(8,128)S(1)}, f32[2,1,256,256]{3,2,1,0:T(8,128)S(1)}) custom-call(bf16[2,512,512]{2,1,0:T(8,128)(2,1)} %a_hbm.1, bf16[2,4,64,256]{3,2,1,0:T(8,128)(2,1)} %panel_hbm.1, bf16[2,4,256,256]{3,2,1,0:T(8,128)(2,1)} %u_hbm.1, f32[2,1,256,256]{3,2,1,0:T(8,128)} %k_hbm.1, s32[4,4]{1,0:T(4,128)} %table_hbm.1), custom_call_target="tpu_custom_call" | custom-call | tf_op jit(solution)/shard_map/pallas_call | solution.py:388
  35.5 1.2 %shard_map.69 = (f32[2,512,256]{2,1,0:T(8,128)}, f32[2,1,256,256]{3,2,1,0:T(8,128)}) custom-call(f32[2,512,256]{2,1,0:T(8,128)S(1)} %get-tuple-element.4.sel, f32[2,1,256,256]{3,2,1,0:T(8,128)S(1)} %get-tuple-element.5.diag), custom_call_target="tpu_custom_call" | custom-call | tf_op jit(solution)/shard_map/pallas_call | solution.py:424

commit v3 on v2

--- a/solution.py
+++ b/solution.py
@@ -34,8 +34,8 @@
 
 def kernel(
     n_rows, n_cols, a_hbm, panel_hbm, u_hbm, k_hbm, table_hbm, sel_out, diag_out,
-    table, av, pv, uv, pr, gather, pick_out, picks, acc, kv, q_own, q_out, q_in, tot,
-    local_sem, p_send, p_recv, a_send, a_recv, g_send, g_recv, q_send, q_recv, t_send, t_recv,
+    table, av, pv, uv, pr, gather, pick_out, picks, acc, kv, z_t, q_own, q_out, q_in, tot,
+    local_sem, p_send, p_recv, a_send, a_recv, g_send, g_recv, d_send, q_recv, t_recv,
 ):
     row = lax.axis_index("prow")
     col = lax.axis_index("pcol")
@@ -65,10 +65,11 @@
     copy_u = pltpu.make_async_copy(u_hbm.at[:, col], uv, local_sem.at[1])
     copy_t = pltpu.make_async_copy(table_hbm, table, local_sem.at[2])
     copy_a = pltpu.make_async_copy(a_hbm, av, local_sem.at[3])
-    copy_k = pltpu.make_async_copy(k_hbm, kv, local_sem.at[4])
+    copy_k = pltpu.make_async_copy(k_hbm, kv, local_sem.at[2])
     copy_p.start()
     copy_u.start()
     copy_t.start()
+    copy_a.start()
 
     barrier = pltpu.get_barrier_semaphore()
 
@@ -84,35 +85,24 @@
     def _():
         greet("prow", over)
 
-    with scope("barrier"):
-        pl.semaphore_wait(barrier, n_cols + 2 - is_end.astype(jnp.int32))
-
     def panel_copy(unit, source):
         return remote(
-            pv.at[:, peer(unit)], pr.at[source], p_send.at[unit], p_recv.at[source], {"pcol": peer(unit)}
+            pv.at[:, peer(unit)], pr.at[source], p_send.at[0], p_recv.at[unit - 1], {"pcol": peer(unit)}
         )
 
     def pick_copy(unit, source):
         return remote(
-            pick_out.at[unit - 1], picks.at[source], a_send.at[unit], a_recv.at[source], {"pcol": peer(unit)}
+            pick_out.at[unit - 1], picks.at[source], a_send.at[0], a_recv.at[unit - 1], {"pcol": peer(unit)}
         )
 
-    def chunk_copy(half, unit, chunk, kind, there):
+    second, whole = 2 * n_cols, 3 * n_cols
+
+    def chunk_copy(half, unit, chunk, index, there):
         block = gather.at[half, unit, chunk]
-        return remote(block, block, g_send.at[kind], g_recv.at[half, unit, chunk], {"prow": there})
-
-    def arrived(half, unit, chunk):
-        chunk_copy(half, unit, chunk, 0, mate).wait_recv()
-
-    with scope("copy_p"):
-        copy_p.wait()
-    copy_a.start()
-    for unit in range(1, n_cols):
-        panel_copy(unit, col).start()
-    copy_k.start()
-    with scope("copy_u"):
-        copy_u.wait()
-        copy_t.wait()
+        return remote(block, block, g_send.at[0], g_recv.at[index], {"prow": there})
+
+    def arrived(view, sem):
+        remote(view, view, sem, sem, {"prow": mate}).wait_recv()
 
     def scale(unit):
         slot = peer(unit)
@@ -128,9 +118,13 @@
                 block = value[plane][:, half * lanes : (half + 1) * lanes]
                 gather[half, unit, row, :, plane * lanes : (plane + 1) * lanes] = (block * live).astype(BF16)
 
-    def spread(half, unit):
-        chunk_copy(half, unit, row, 0, over).start()
-        chunk_copy(half, unit, row, 1, mate).start()
+    def send_over(half, unit):
+        index = second + unit if half else unit + jnp.where(is_end, n_cols, 0)
+        chunk_copy(half, unit, row, index, over).start()
+
+    def send_mate(half, unit):
+        index = jnp.where(is_end, whole + half, second * half + unit)
+        chunk_copy(half, unit, row, index, mate).start()
 
     def pick(unit):
         node = peer(unit)
@@ -148,11 +142,36 @@
             else:
                 pick_out[unit - 1, plane] = total
 
-    for unit in range(2):
-        with scope(f"scale{unit}"):
-            scale(unit)
-        for half in range(2):
-            spread(half, unit)
+    with scope("copies"):
+        copy_p.wait()
+        copy_u.wait()
+        copy_t.wait()
+    copy_k.start()
+    with scope("scale0"):
+        scale(0)
+    with scope("barrier"):
+        pl.semaphore_wait(barrier, n_cols + 2 - is_end.astype(jnp.int32))
+    for unit in range(1, n_cols):
+        panel_copy(unit, col).start()
+    send_over(0, 0)
+    send_mate(0, 0)
+    with scope("scale1"):
+        scale(1)
+    send_over(0, 1)
+    send_mate(0, 1)
+    far_home = unit_of(far)
+    early = jnp.where(far_home < 2, far_home, 0)
+    send_over(1, early)
+
+    @pl.when(is_end)
+    def _():
+        send_mate(1, early)
+
+    @pl.when(is_inner)
+    def _():
+        send_mate(1, 0)
+        send_mate(1, 1)
+
     with scope("copy_a"):
         copy_a.wait()
     for unit in list(range(2, n_cols)) + [1]:
@@ -162,55 +181,78 @@
     pick(0)
     late = range(2, n_cols)
 
-    def relay(half, unit, chunk, kind):
-        arrived(half, unit, chunk)
-        chunk_copy(half, unit, chunk, kind, end).start()
+    def relay(unit, chunk, index):
+        arrived(gather.at[0, unit, chunk], g_recv.at[index])
+        chunk_copy(0, unit, chunk, unit, end).start()
 
     @pl.when(is_end)
     def _():
         for unit in late:
             with scope(f"scale{unit}"):
                 scale(unit)
-            spread(0, unit)
-        for unit in late:
-            spread(1, unit)
+            send_over(0, unit)
+            send_mate(0, unit)
+        for i in range(n_cols):
+            unit = (far_home + i) % n_cols
+
+            @pl.when(unit != early)
+            def _():
+                send_over(1, unit)
+                send_mate(1, unit)
 
     @pl.when(is_inner)
     def _():
         with scope("scale2"):
             scale(2)
-        spread(0, 2)
+        send_over(0, 2)
+        send_mate(0, 2)
         with scope("relay_0o"):
-            relay(0, 0, over, 2)
+            relay(0, over, 0)
         with scope("relay_1o"):
-            relay(0, 1, over, 2)
+            relay(1, over, 1)
         with scope("scale3"):
             scale(3)
-        spread(0, 3)
+        send_over(0, 3)
+        send_mate(0, 3)
         with scope("relay_01f"):
-            relay(0, 0, far, 3)
-            relay(0, 1, far, 3)
-        for unit in late:
-            spread(1, unit)
+            relay(0, far, n_cols)
+            relay(1, far, n_cols + 1)
+        for i in range(n_cols):
+            unit = (far_home + i) % n_cols
+
+            @pl.when(unit != early)
+            def _():
+                send_over(1, unit)
+
+        home = unit_of(end)
+
+        @pl.when(home >= 2)
+        def _():
+            send_mate(1, home)
+
         for unit in late:
             with scope(f"relay_{unit}o"):
-                relay(0, unit, over, 2)
+                relay(unit, over, unit)
             with scope(f"relay_{unit}f"):
-                relay(0, unit, far, 3)
+                relay(unit, far, n_cols + unit)
         for i in range(n_cols):
-            unit = (unit_of(end) + i) % n_cols
-            with scope(f"relay_h1_{i}o"):
-                relay(1, unit, over, 2)
-            with scope(f"relay_h1_{i}f"):
-                relay(1, unit, far, 3)
+            if i == 1:
+                for unit in late:
+
+                    @pl.when(unit != home)
+                    def _():
+                        send_mate(1, unit)
+
+            unit = (home + i) % n_cols
+            with scope(f"relay_h1_{i}"):
+                arrived(gather.at[1, unit, 0:2], g_recv.at[second + unit])
+            chunk_copy(1, unit, over, second + unit, end).start()
+            chunk_copy(1, unit, far, second + unit, end).start()
 
     def ready(half, unit):
         @pl.when(is_end)
         def _():
-            arrived(half, unit, over)
-            arrived(half, unit, far)
-
-        arrived(half, unit, mate)
+            arrived(gather.at[half, unit, 0 : n_rows - 1], g_recv.at[second * half + unit])
 
     def multiply(half, unit, first):
         right = gather[half, unit].reshape(width, width)
@@ -222,18 +264,22 @@
             else:
                 acc[plane] += value
 
+    @pl.when(is_inner)
+    def _():
+        for half in range(2):
+            with scope(f"mate{half}"):
+                arrived(gather.at[half, 0], g_recv.at[whole + half])
+
     home = unit_of(row)
     live = (jnp.full((1, width), table[col, row]) >= 0).astype(F32)
     named = jnp.full((1, lanes), table[col, row]) - row * row_blocks
 
-    def owner(band):
-        return n_rows // 2 - 1 + band // share
+    first = n_rows // 2 - 1
 
     def quad_copy(half, there, part, source):
-        band = (there - (n_rows // 2 - 1)) * share + part
         return remote(
-            q_out.at[half, band], q_in.at[source, half, part], q_send.at[0], q_recv.at[source, half, part],
-            {"prow": there},
+            q_out.at[half, (there - first) * share + part], q_in.at[source, half, part],
+            d_send.at[0], q_recv.at[half, part], {"prow": there},
         )
 
     def quad(half):
@@ -241,28 +287,22 @@
         imag = acc[0, :, lanes:] + acc[1, :, :lanes]
         value = jnp.concatenate([real, imag], axis=1) * live
         low = value.astype(BF16)
-        for top in range(2):
-            z = gather[top, home].reshape(width, width)
-            product = lax.dot_general(z, low, (((0,), (0,)), ((), ())), preferred_element_type=F32)
+        for there in (over, inner):
+            top = there - first
+            product = jnp.dot(z_t[top], low, preferred_element_type=F32)
             real = product[:lanes, :lanes] - product[lanes:, lanes:]
             imag = product[:lanes, lanes:] + product[lanes:, :lanes]
-            whole = jnp.concatenate([real, imag], axis=1)
-            for i in range(bands // 2):
-                block = whole[i * band_rows : (i + 1) * band_rows]
-                band = top * (bands // 2) + i
-                q_out[half, band] = block.astype(BF16)
-
-                @pl.when(row == owner(band))
-                def _():
-                    q_own[half, band % share] = block
-
-        for part in range(share):
-            quad_copy(half, over, part, row).start()
-
-        @pl.when(is_end)
-        def _():
+            both = jnp.concatenate([real, imag], axis=1)
             for part in range(share):
-                quad_copy(half, mate, part, row).start()
+                block = both[part * band_rows : (part + 1) * band_rows]
+                q_out[half, top * share + part] = block.astype(BF16)
+                if there is inner:
+                    q_own[half, part] = block
+
+            @pl.when(row != there)
+            def _():
+                for part in range(share):
+                    quad_copy(half, there, part, row).start()
 
         columns = slice(half * lanes, (half + 1) * lanes)
         for i in range(row_blocks):
@@ -280,6 +320,8 @@
         multiply(0, unit, unit == 0)
     with scope("ready_home"):
         ready(1, home)
+    for top in range(2):
+        z_t[top] = gather[top, home].reshape(width, width).T
     with scope("quad0"):
         quad(0)
     for i in range(n_cols):
@@ -292,72 +334,65 @@
         quad(1)
     copy_k.wait()
 
-    def total_copy(half, band, kind, there):
-        block = tot.at[half, band]
-        return remote(block, block, t_send.at[kind], t_recv.at[half, band], {"prow": there})
-
-    def finish(half, band):
-        rows = pl.ds(pl.multiple_of(band * band_rows, band_rows), band_rows)
+    def drain(view, sem):
+        remote(view, view, sem, sem, {"prow": mate}).wait_send()
+
+    drain(pr.at[0 : n_cols - 1], p_send.at[0])
+    drain(pick_out, a_send.at[0])
+
+    @pl.when(is_inner)
+    def _():
+        drain(gather, g_send.at[0])
+
+    @pl.when(is_end)
+    def _():
+        drain(gather.at[0], g_send.at[0])
+        drain(q_out, d_send.at[0])
+
+    def total_copy(half, part, there):
+        block = tot.at[half, (row - first) * share + part]
+        return remote(block, block, d_send.at[0], t_recv.at[half, row - first], {"prow": there})
+
+    def finish(half, group):
         columns = slice(half * lanes, (half + 1) * lanes)
-        for plane in range(2):
-            block = tot[half, band, :, plane * lanes : (plane + 1) * lanes].astype(F32)
-            diag_out[plane, 0, rows, columns] = kv[plane, 0, rows, columns] + block
-
-    near_band = (inner - (n_rows // 2 - 1)) * share
-    over_band = (over - (n_rows // 2 - 1)) * share
+        for part in range(share):
+            band = group * share + part
+            rows = pl.ds(pl.multiple_of(band * band_rows, band_rows), band_rows)
+            for plane in range(2):
+                block = tot[half, band, :, plane * lanes : (plane + 1) * lanes].astype(F32)
+                diag_out[plane, 0, rows, columns] = kv[plane, 0, rows, columns] + block
 
     @pl.when(is_inner)
     def _():
         for half in range(2):
             for part in range(share):
                 with scope(f"wq{half}_{part}"):
-                    for source in (over, end, far):
-                        quad_copy(half, row, part, source).wait_recv()
+                    arrived(q_in.at[0 : n_rows - 1, half, part], q_recv.at[half, part])
                 total = q_own[half, part]
                 for source in (over, end, far):
                     total = total + q_in[source, half, part].astype(F32)
-                tot[half, near_band + part] = total.astype(BF16)
-                total_copy(half, near_band + part, 0, far).start()
-                total_copy(half, near_band + part, 1, end).start()
-                total_copy(half, near_band + part, 2, over).start()
+                tot[half, (row - first) * share + part] = total.astype(BF16)
+                total_copy(half, part, far).start()
+                total_copy(half, part, end).start()
+            for part in range(share):
+                total_copy(half, part, over).start()
         for half in range(2):
-            for part in range(share):
-                finish(half, near_band + part)
+            finish(half, row - first)
 
     for half in range(2):
         @pl.when(is_end)
         def _():
-            for part in range(share):
-                with scope(f"wt_near{half}_{part}"):
-                    total_copy(half, near_band + part, 0, mate).wait_recv()
-                finish(half, near_band + part)
-
-        for part in range(share):
-            with scope(f"wt_over{half}_{part}"):
-                total_copy(half, over_band + part, 0, mate).wait_recv()
-            finish(half, over_band + part)
-
-    for unit in range(1, n_cols):
-        panel_copy(unit, col).wait_send()
-        pick_copy(unit, col).wait_send()
-
-    def drain(view, sem):
-        remote(view, view, sem, sem, {"prow": mate}).wait_send()
-
-    drain(gather.at[0, 0:2], g_send.at[0])
-    drain(gather.at[0, 0:2], g_send.at[1])
-
-    @pl.when(is_end)
-    def _():
-        drain(q_out, q_send.at[0])
-
-    @pl.when(is_inner)
-    def _():
-        drain(gather.at[0, 0:2], g_send.at[2])
-        drain(gather.at[0, 0:2], g_send.at[3])
-        drain(q_out.at[0], q_send.at[0])
-        for kind in range(3):
-            drain(tot.at[0], t_send.at[kind])
+            with scope(f"wt_near{half}"):
+                arrived(tot.at[half, 0:share], t_recv.at[half, inner - first])
+            finish(half, inner - first)
+
+        with scope(f"wt_over{half}"):
+            arrived(tot.at[half, 0:share], t_recv.at[half, over - first])
+        finish(half, over - first)
+
+    @pl.when(is_inner)
+    def _():
+        drain(q_in, d_send.at[0])
 
 
 def place(sel, diag, sel_out, diag_out, out_sem):
@@ -401,21 +436,21 @@
             pltpu.VMEM((n_cols, 2, width, width), BF16),
             pltpu.VMEM((2, width, width), F32),
             pltpu.VMEM(k_inv.shape, F32),
+            pltpu.VMEM((2, width, width), BF16),
             pltpu.VMEM((2, share) + piece, F32),
             pltpu.VMEM((2, bands) + piece, BF16),
             pltpu.VMEM((n_rows, 2, share) + piece, BF16),
             pltpu.VMEM((2, bands) + piece, BF16),
-            dma((5,)),
-            dma((n_cols,)),
-            dma((n_cols,)),
-            dma((n_cols,)),
-            dma((n_cols,)),
             dma((4,)),
-            dma((2, n_cols, n_rows)),
             dma((1,)),
-            dma((n_rows, 2, share)),
-            dma((3,)),
-            dma((2, bands)),
+            dma((n_cols - 1,)),
+            dma((1,)),
+            dma((n_cols - 1,)),
+            dma((1,)),
+            dma((3 * n_cols + 2,)),
+            dma((1,)),
+            dma((2, share)),
+            dma((2, 2)),
         ],
         compiler_params=pltpu.CompilerParams(
             collective_id=0, has_side_effects=True

time: 36.8 us -> 35.8 us (0.973)
  Pallas kernels: 36 us -> 35.1 us
    pallas_call x1, Pallas kernels: 34.8 us -> 33.9 us  [compact(): pl.pallas_call(functools.partial(kernel, n_rows, n_cols), out_shape=tuple...]
where the time goes in v3:
time: 35.8 us; the launch traced here: 35.7 us
  Pallas kernels  35.1 us (98%)
  between operations  0.64 us (2%)
    pallas_call x1, Pallas kernels, compact(): pl.pallas_call(functools.partial(kernel, n_rows, n_cols), out_shape=tuple...  33.9 us
    pallas_call x1, Pallas kernels, compact(): pl.pallas_call(place, out_shape=shapes, in_specs=[vmem, vmem], out_specs=...  1.16 us

profile of v3, /device:TPU:0, one launch (start us, length us, event | category | flops | bytes accessed | tf_op | source)
XLA Modules:
  0.0 35.7 jit_solution(8556068823791886450)
XLA Ops:
  0.6 33.9 %shard_map.68 = (f32[2,512,256]{2,1,0:T(8,128)S(1)}, f32[2,1,256,256]{3,2,1,0:T(8,128)S(1)}) custom-call(bf16[2,512,512]{2,1,0:T(8,128)(2,1)} %a_hbm.1, bf16[2,4,64,256]{3,2,1,0:T(8,128)(2,1)} %panel_hbm.1, bf16[2,4,256,256]{3,2,1,0:T(8,128)(2,1)} %u_hbm.1, f32[2,1,256,256]{3,2,1,0:T(8,128)} %k_hbm.1, s32[4,4]{1,0:T(4,128)} %table_hbm.1), custom_call_target="tpu_custom_call" | custom-call | tf_op jit(solution)/shard_map/pallas_call | solution.py:423
  34.5 1.2 %shard_map.69 = (f32[2,512,256]{2,1,0:T(8,128)}, f32[2,1,256,256]{3,2,1,0:T(8,128)}) custom-call(f32[2,512,256]{2,1,0:T(8,128)S(1)} %get-tuple-element.4.sel, f32[2,1,256,256]{3,2,1,0:T(8,128)S(1)} %get-tuple-element.5.diag), custom_call_target="tpu_custom_call" | custom-call | tf_op jit(solution)/shard_map/pallas_call | solution.py:459

commit v4 on v3

--- a/solution.py
+++ b/solution.py
@@ -202,12 +202,12 @@
 
     @pl.when(is_inner)
     def _():
+        with scope("relay_0o"):
+            relay(0, over, 0)
         with scope("scale2"):
             scale(2)
         send_over(0, 2)
         send_mate(0, 2)
-        with scope("relay_0o"):
-            relay(0, over, 0)
         with scope("relay_1o"):
             relay(1, over, 1)
         with scope("scale3"):
@@ -374,6 +374,7 @@
                 tot[half, (row - first) * share + part] = total.astype(BF16)
                 total_copy(half, part, far).start()
                 total_copy(half, part, end).start()
+        for half in range(2):
             for part in range(share):
                 total_copy(half, part, over).start()
         for half in range(2):

time: 35.8 us -> 35.4 us (0.989)
  Pallas kernels: 35.1 us -> 34.6 us
    pallas_call x1, Pallas kernels: 33.9 us -> 33.5 us  [compact(): pl.pallas_call(functools.partial(kernel, n_rows, n_cols), out_shape=tuple...]
where the time goes in v4:
time: 35.4 us; the launch traced here: 35.3 us
  Pallas kernels  34.6 us (98%)
  between operations  0.64 us (2%)
    pallas_call x1, Pallas kernels, compact(): pl.pallas_call(functools.partial(kernel, n_rows, n_cols), out_shape=tuple...  33.5 us
    pallas_call x1, Pallas kernels, compact(): pl.pallas_call(place, out_shape=shapes, in_specs=[vmem, vmem], out_specs=...  1.16 us

profile of v4, /device:TPU:0, one launch (start us, length us, event | category | flops | bytes accessed | tf_op | source)
XLA Modules:
  0.0 35.3 jit_solution(5374615488954872361)
XLA Ops:
  0.6 33.5 %shard_map.68 = (f32[2,512,256]{2,1,0:T(8,128)S(1)}, f32[2,1,256,256]{3,2,1,0:T(8,128)S(1)}) custom-call(bf16[2,512,512]{2,1,0:T(8,128)(2,1)} %a_hbm.1, bf16[2,4,64,256]{3,2,1,0:T(8,128)(2,1)} %panel_hbm.1, bf16[2,4,256,256]{3,2,1,0:T(8,128)(2,1)} %u_hbm.1, f32[2,1,256,256]{3,2,1,0:T(8,128)} %k_hbm.1, s32[4,4]{1,0:T(4,128)} %table_hbm.1), custom_call_target="tpu_custom_call" | custom-call | tf_op jit(solution)/shard_map/pallas_call | solution.py:424
  34.1 1.2 %shard_map.69 = (f32[2,512,256]{2,1,0:T(8,128)}, f32[2,1,256,256]{3,2,1,0:T(8,128)}) custom-call(f32[2,512,256]{2,1,0:T(8,128)S(1)} %get-tuple-element.4.sel, f32[2,1,256,256]{3,2,1,0:T(8,128)S(1)} %get-tuple-element.5.diag), custom_call_target="tpu_custom_call" | custom-call | tf_op jit(solution)/shard_map/pallas_call | solution.py:460

commit v5 on v4

--- a/solution.py
+++ b/solution.py
@@ -9,6 +9,7 @@
 
 BF16 = jnp.bfloat16
 F32 = jnp.float32
+LANES = 128
 scope = jax.named_scope
 
 
@@ -32,21 +33,47 @@
     )
 
 
+def swap(x):
+    return pltpu.roll(x, x.shape[1] // 2, 1)
+
+
+def low_lanes():
+    return lax.broadcasted_iota(jnp.int32, (1, LANES), 1) < LANES // 2
+
+
+def tiles_of(x):
+    return [x[:, at : at + LANES] for at in range(0, x.shape[1], LANES)]
+
+
+def join(left, right):
+    sign = jnp.where(low_lanes(), -1.0, 1.0)
+    return jnp.concatenate([a + swap(b) * sign for a, b in zip(tiles_of(left), tiles_of(right))], axis=1)
+
+
+def cross(a, b):
+    low = low_lanes()
+    return jnp.where(low, a, swap(b)), jnp.where(low, swap(a), b)
+
+
 def kernel(
-    n_rows, n_cols, a_hbm, panel_hbm, u_hbm, k_hbm, table_hbm, sel_out, diag_out,
-    table, av, pv, uv, pr, gather, pick_out, picks, acc, kv, z_t, q_own, q_out, q_in, tot,
+    n_rows, n_cols, spans, a_hbm, panel_hbm, u_hbm, k_hbm, table_hbm, sel_out, diag_out,
+    table, av, pv, uv, pr, pick_out, picks, acc, kv, z_t,
+    gather_0, gather_1, gather_2, own_0, own_1, own_2, out_0, out_1, out_2,
+    in_0, in_1, in_2, tot_0, tot_1, tot_2,
     local_sem, p_send, p_recv, a_send, a_recv, g_send, g_recv, d_send, q_recv, t_recv,
 ):
+    gather, own = (gather_0, gather_1, gather_2), (own_0, own_1, own_2)
+    q_out, q_in, tot = (out_0, out_1, out_2), (in_0, in_1, in_2), (tot_0, tot_1, tot_2)
+    groups = range(len(spans))
     row = lax.axis_index("prow")
     col = lax.axis_index("pcol")
     width = u_hbm.shape[-1]
     pairs = n_cols // 2
     row_blocks = a_hbm.shape[1] // width
     col_blocks = a_hbm.shape[2] // width
-    lanes = width // 2
-    share = q_in.shape[2]
-    band_rows = q_in.shape[3]
-    bands = q_out.shape[1]
+    band_rows = LANES // 2
+    share = q_in[0].shape[1]
+    first = n_rows // 2 - 1
     mate = row + 1 - 2 * (row % 2)
     is_end = (row == 0) | (row == n_rows - 1)
     is_inner = jnp.logical_not(is_end)
@@ -95,14 +122,20 @@
             pick_out.at[unit - 1], picks.at[source], a_send.at[0], a_recv.at[unit - 1], {"pcol": peer(unit)}
         )
 
-    second, whole = 2 * n_cols, 3 * n_cols
-
-    def chunk_copy(half, unit, chunk, index, there):
-        block = gather.at[half, unit, chunk]
+    def base(group):
+        return (group + 1) * n_cols if group else 0
+
+    all_mate = 4 * n_cols
+
+    def chunk_copy(group, unit, chunk, index, there):
+        block = gather[group].at[unit, chunk]
         return remote(block, block, g_send.at[0], g_recv.at[index], {"prow": there})
 
     def arrived(view, sem):
         remote(view, view, sem, sem, {"prow": mate}).wait_recv()
+
+    def drain(view, sem):
+        remote(view, view, sem, sem, {"prow": mate}).wait_send()
 
     def scale(unit):
         slot = peer(unit)
@@ -111,20 +144,23 @@
         else:
             panel_copy(unit, slot).wait_recv()
             left = (pr[slot, 0], pr[slot, 1])
-        value = cdot(left, (uv[0], uv[1]))
-        live = (jnp.full((1, lanes), table[col, slot]) >= 0).astype(F32)
-        for half in range(2):
-            for plane in range(2):
-                block = value[plane][:, half * lanes : (half + 1) * lanes]
-                gather[half, unit, row, :, plane * lanes : (plane + 1) * lanes] = (block * live).astype(BF16)
-
-    def send_over(half, unit):
-        index = second + unit if half else unit + jnp.where(is_end, n_cols, 0)
-        chunk_copy(half, unit, row, index, over).start()
-
-    def send_mate(half, unit):
-        index = jnp.where(is_end, whole + half, second * half + unit)
-        chunk_copy(half, unit, row, index, mate).start()
+        real, imag = cdot(left, (uv[0], uv[1]))
+        live = (jnp.full((1, width), table[col, slot]) >= 0).astype(F32)
+        packed = []
+        for a, b in zip(tiles_of(real * live), tiles_of(imag * live)):
+            packed.extend(cross(a, b))
+        for group in groups:
+            lo, hi = spans[group]
+            for tile in range(lo, hi):
+                at = (tile - lo) * LANES
+                gather[group][unit, row, :, at : at + LANES] = packed[tile].astype(BF16)
+
+    def send_over(group, unit):
+        index = base(group) + unit if group else unit + jnp.where(is_end, n_cols, 0)
+        chunk_copy(group, unit, row, index, over).start()
+
+    def send_mate(group, unit):
+        chunk_copy(group, unit, row, jnp.where(is_end, all_mate, base(group) + unit), mate).start()
 
     def pick(unit):
         node = peer(unit)
@@ -161,16 +197,19 @@
     send_mate(0, 1)
     far_home = unit_of(far)
     early = jnp.where(far_home < 2, far_home, 0)
-    send_over(1, early)
+    for group in groups[1:]:
+        send_over(group, early)
 
     @pl.when(is_end)
     def _():
-        send_mate(1, early)
+        for group in groups[1:]:
+            send_mate(group, early)
 
     @pl.when(is_inner)
     def _():
-        send_mate(1, 0)
-        send_mate(1, 1)
+        for unit in range(2):
+            for group in groups[1:]:
+                send_mate(group, unit)
 
     with scope("copy_a"):
         copy_a.wait()
@@ -180,10 +219,17 @@
         pick_copy(unit, col).start()
     pick(0)
     late = range(2, n_cols)
+    order = [(group, 0) for group in groups[1:]] + [(group, i) for group in groups[1:] for i in range(1, n_cols)]
 
     def relay(unit, chunk, index):
-        arrived(gather.at[0, unit, chunk], g_recv.at[index])
+        arrived(gather[0].at[unit, chunk], g_recv.at[index])
         chunk_copy(0, unit, chunk, unit, end).start()
+
+    def relay_both(group, unit):
+        index = base(group) + unit
+        arrived(gather[group].at[unit, 0:2], g_recv.at[index])
+        chunk_copy(group, unit, over, index, end).start()
+        chunk_copy(group, unit, far, index, end).start()
 
     @pl.when(is_end)
     def _():
@@ -192,13 +238,13 @@
                 scale(unit)
             send_over(0, unit)
             send_mate(0, unit)
-        for i in range(n_cols):
+        for group, i in order:
             unit = (far_home + i) % n_cols
 
             @pl.when(unit != early)
             def _():
-                send_over(1, unit)
-                send_mate(1, unit)
+                send_over(group, unit)
+                send_mate(group, unit)
 
     @pl.when(is_inner)
     def _():
@@ -217,183 +263,211 @@
         with scope("relay_01f"):
             relay(0, far, n_cols)
             relay(1, far, n_cols + 1)
-        for i in range(n_cols):
+        for group, i in order:
             unit = (far_home + i) % n_cols
 
             @pl.when(unit != early)
             def _():
-                send_over(1, unit)
+                send_over(group, unit)
 
         home = unit_of(end)
 
         @pl.when(home >= 2)
         def _():
-            send_mate(1, home)
+            for group in groups[1:]:
+                send_mate(group, home)
 
         for unit in late:
             with scope(f"relay_{unit}o"):
                 relay(unit, over, unit)
             with scope(f"relay_{unit}f"):
                 relay(unit, far, n_cols + unit)
-        for i in range(n_cols):
+        for group, i in order:
             if i == 1:
                 for unit in late:
 
                     @pl.when(unit != home)
                     def _():
-                        send_mate(1, unit)
-
-            unit = (home + i) % n_cols
-            with scope(f"relay_h1_{i}"):
-                arrived(gather.at[1, unit, 0:2], g_recv.at[second + unit])
-            chunk_copy(1, unit, over, second + unit, end).start()
-            chunk_copy(1, unit, far, second + unit, end).start()
-
-    def ready(half, unit):
+                        send_mate(group, unit)
+
+            with scope(f"relay_g{group}_{i}"):
+                relay_both(group, (home + i) % n_cols)
+        with scope("mate"):
+            arrived(picks.at[0], g_recv.at[all_mate])
+
+    def ready(group, unit):
         @pl.when(is_end)
         def _():
-            arrived(gather.at[half, unit, 0 : n_rows - 1], g_recv.at[second * half + unit])
-
-    def multiply(half, unit, first):
-        right = gather[half, unit].reshape(width, width)
+            arrived(gather[group].at[unit, 0 : n_rows - 1], g_recv.at[base(group) + unit])
+
+    def span(group):
+        lo, hi = spans[group]
+        return slice(lo * LANES, hi * LANES)
+
+    def multiply(group, unit, start):
+        right = gather[group][unit].reshape(width, gather[group].shape[-1])
         slot = peer(unit)
         for plane in range(2):
             value = jnp.dot(picks[slot, plane], right, preferred_element_type=F32)
-            if first:
-                acc[plane] = value
+            if start:
+                acc[plane, :, span(group)] = value
             else:
-                acc[plane] += value
-
-    @pl.when(is_inner)
-    def _():
-        for half in range(2):
-            with scope(f"mate{half}"):
-                arrived(gather.at[half, 0], g_recv.at[whole + half])
+                acc[plane, :, span(group)] += value
 
     home = unit_of(row)
-    live = (jnp.full((1, width), table[col, row]) >= 0).astype(F32)
-    named = jnp.full((1, lanes), table[col, row]) - row * row_blocks
-
-    first = n_rows // 2 - 1
-
-    def quad_copy(half, there, part, source):
+    live = (jnp.full((1, LANES), table[col, row]) >= 0).astype(F32)
+    named = jnp.full((1, LANES), table[col, row]) - row * row_blocks
+
+    def pieces(group):
+        return [(part, 1) for part in range(share)] if group == 0 else [(0, share)]
+
+    def quad_copy(group, there, piece, source):
+        part, count = piece
+        at = (there - first) * share + part
         return remote(
-            q_out.at[half, (there - first) * share + part], q_in.at[source, half, part],
-            d_send.at[0], q_recv.at[half, part], {"prow": there},
+            q_out[group].at[pl.ds(at, count)], q_in[group].at[source, part : part + count],
+            d_send.at[0], q_recv.at[group + share - 1 if group else part], {"prow": there},
         )
 
-    def quad(half):
-        real = acc[0, :, :lanes] - acc[1, :, lanes:]
-        imag = acc[0, :, lanes:] + acc[1, :, :lanes]
-        value = jnp.concatenate([real, imag], axis=1) * live
+    def quad(group):
+        value = join(acc[0, :, span(group)], acc[1, :, span(group)])
+        value = jnp.concatenate([x * live for x in tiles_of(value)], axis=1)
+        acc[0, :, span(group)] = value
         low = value.astype(BF16)
         for there in (over, inner):
             top = there - first
             product = jnp.dot(z_t[top], low, preferred_element_type=F32)
-            real = product[:lanes, :lanes] - product[lanes:, lanes:]
-            imag = product[:lanes, lanes:] + product[lanes:, :lanes]
-            both = jnp.concatenate([real, imag], axis=1)
             for part in range(share):
-                block = both[part * band_rows : (part + 1) * band_rows]
-                q_out[half, top * share + part] = block.astype(BF16)
+                at = part * LANES
+                block = join(product[at : at + band_rows], product[at + band_rows : at + LANES])
+                q_out[group][top * share + part] = block.astype(BF16)
                 if there is inner:
-                    q_own[half, part] = block
-
-            @pl.when(row != there)
+                    own[group][part] = block
+
+            if there is over:
+                quad_copy(group, over, pieces(group)[0], row).start()
+
+        for number, piece in enumerate(pieces(group)):
+            if number > 0:
+                quad_copy(group, over, piece, row).start()
+
+            @pl.when(is_end)
             def _():
-                for part in range(share):
-                    quad_copy(half, there, part, row).start()
-
-        columns = slice(half * lanes, (half + 1) * lanes)
-        for i in range(row_blocks):
-            keep = -(named == i).astype(F32)
-            for plane in range(2):
-                block = value[:, plane * lanes : (plane + 1) * lanes]
-                sel_out[plane, i * width : (i + 1) * width, columns] = block * keep
+                quad_copy(group, mate, piece, row).start()
 
     for unit in range(n_cols):
-        with scope(f"ready_h0_{unit}"):
+        with scope(f"ready_g0_{unit}"):
             ready(0, unit)
+        if unit == n_cols - 1:
+            with scope("ready_home"):
+                for group in groups[1:]:
+                    ready(group, home)
+            for group in groups:
+                turned = gather[group][home].reshape(width, gather[group].shape[-1]).T
+                for tile in range(*spans[group]):
+                    at = (tile - spans[group][0]) * LANES
+                    to = (tile % share) * LANES
+                    z_t[tile // share, to : to + LANES, :] = turned[at : at + LANES]
         with scope(f"wpick_{unit}"):
             if unit > 0:
                 pick_copy(unit, peer(unit)).wait_recv()
         multiply(0, unit, unit == 0)
-    with scope("ready_home"):
-        ready(1, home)
-    for top in range(2):
-        z_t[top] = gather[top, home].reshape(width, width).T
     with scope("quad0"):
         quad(0)
-    for i in range(n_cols):
-        unit = (home + i) % n_cols
-        if i > 0:
-            with scope(f"ready_h1_{i}"):
-                ready(1, unit)
-        multiply(1, unit, i == 0)
-    with scope("quad1"):
-        quad(1)
+    for group in groups[1:]:
+        for i in range(n_cols):
+            unit = (home + i) % n_cols
+            if i > 0:
+                with scope(f"ready_g{group}_{i}"):
+                    ready(group, unit)
+            multiply(group, unit, i == 0)
+        with scope(f"quad{group}"):
+            quad(group)
+
+    for pair in range(width // LANES):
+        at = 2 * pair * LANES
+        planes = cross(acc[0, :, at : at + LANES], acc[0, :, at + LANES : at + 2 * LANES])
+        columns = slice(pair * LANES, (pair + 1) * LANES)
+        for i in range(row_blocks):
+            keep = -(named == i).astype(F32)
+            for plane in range(2):
+                sel_out[plane, i * width : (i + 1) * width, columns] = planes[plane] * keep
     copy_k.wait()
-
-    def drain(view, sem):
-        remote(view, view, sem, sem, {"prow": mate}).wait_send()
-
     drain(pr.at[0 : n_cols - 1], p_send.at[0])
     drain(pick_out, a_send.at[0])
 
     @pl.when(is_inner)
     def _():
-        drain(gather, g_send.at[0])
+        drain(picks, g_send.at[0])
 
     @pl.when(is_end)
     def _():
-        drain(gather.at[0], g_send.at[0])
-        drain(q_out, d_send.at[0])
-
-    def total_copy(half, part, there):
-        block = tot.at[half, (row - first) * share + part]
-        return remote(block, block, d_send.at[0], t_recv.at[half, row - first], {"prow": there})
-
-    def finish(half, group):
-        columns = slice(half * lanes, (half + 1) * lanes)
+        drain(picks.at[0:2], g_send.at[0])
+        drain(picks.at[0], d_send.at[0])
+
+    def total_copy(group, piece, there):
+        part, count = piece
+        block = tot[group].at[pl.ds((row - first) * share + part, count)]
+        return remote(block, block, d_send.at[0], t_recv.at[group * 2 + row - first], {"prow": there})
+
+    where_tile = {tile: group for group in groups for tile in range(*spans[group])}
+
+    def tile_of(tile, band):
+        group = where_tile[tile]
+        at = (tile - spans[group][0]) * LANES
+        return tot[group][band, :, at : at + LANES].astype(F32)
+
+    def finish(pair, owner):
+        columns = slice(pair * LANES, (pair + 1) * LANES)
         for part in range(share):
-            band = group * share + part
+            band = owner * share + part
             rows = pl.ds(pl.multiple_of(band * band_rows, band_rows), band_rows)
+            planes = cross(tile_of(2 * pair, band), tile_of(2 * pair + 1, band))
             for plane in range(2):
-                block = tot[half, band, :, plane * lanes : (plane + 1) * lanes].astype(F32)
-                diag_out[plane, 0, rows, columns] = kv[plane, 0, rows, columns] + block
+                diag_out[plane, 0, rows, columns] = kv[plane, 0, rows, columns] + planes[plane]
 
     @pl.when(is_inner)
     def _():
-        for half in range(2):
-            for part in range(share):
-                with scope(f"wq{half}_{part}"):
-                    arrived(q_in.at[0 : n_rows - 1, half, part], q_recv.at[half, part])
-                total = q_own[half, part]
-                for source in (over, end, far):
-                    total = total + q_in[source, half, part].astype(F32)
-                tot[half, (row - first) * share + part] = total.astype(BF16)
-                total_copy(half, part, far).start()
-                total_copy(half, part, end).start()
-        for half in range(2):
-            for part in range(share):
-                total_copy(half, part, over).start()
-        for half in range(2):
-            finish(half, row - first)
-
-    for half in range(2):
-        @pl.when(is_end)
-        def _():
-            with scope(f"wt_near{half}"):
-                arrived(tot.at[half, 0:share], t_recv.at[half, inner - first])
-            finish(half, inner - first)
-
-        with scope(f"wt_over{half}"):
-            arrived(tot.at[half, 0:share], t_recv.at[half, over - first])
-        finish(half, over - first)
+        for group in groups:
+            for piece in pieces(group):
+                part, count = piece
+                with scope(f"wq{group}_{part}"):
+                    arrived(
+                        q_in[group].at[0 : n_rows - 1, part : part + count],
+                        q_recv.at[group + share - 1 if group else part],
+                    )
+                for at in range(part, part + count):
+                    total = own[group][at]
+                    for source in (over, end, far):
+                        total = total + q_in[group][source, at].astype(F32)
+                    tot[group][(row - first) * share + at] = total.astype(BF16)
+                total_copy(group, piece, far).start()
+                total_copy(group, piece, end).start()
+        for group in groups:
+            total_copy(group, (0, share), over).start()
+        for pair in range(width // LANES):
+            finish(pair, row - first)
+
+    def total_wait(group, owner):
+        arrived(tot[group].at[0:share], t_recv.at[group * 2 + owner])
+
+    @pl.when(is_end)
+    def _():
+        for group in groups:
+            for there in (inner, over):
+                with scope(f"wt{group}"):
+                    total_wait(group, there - first)
+                if group != 1:
+                    finish(1 if group else 0, there - first)
 
     @pl.when(is_inner)
     def _():
-        drain(q_in, d_send.at[0])
+        for group in groups:
+            with scope(f"wt{group}"):
+                total_wait(group, over - first)
+        for pair in range(width // LANES):
+            finish(pair, over - first)
+        drain(picks.at[0:2], d_send.at[0])
 
 
 def place(sel, diag, sel_out, diag_out, out_sem):
@@ -411,8 +485,9 @@
     n_rows, n_cols = lax.axis_size("prow"), lax.axis_size("pcol")
     width, part = u_inv.shape[-1], panel.shape[2]
     row_blocks = ainv_anc.shape[1] // width
-    bands = n_rows
-    share = bands // 2
+    tiles = 2 * width // LANES
+    share = tiles // 2
+    spans = ((0, share), (share, share + share // 2), (share + share // 2, tiles))
     hbm = pl.BlockSpec(memory_space=pltpu.HBM)
     vmem = pl.BlockSpec(memory_space=pltpu.VMEM)
     dma = pltpu.SemaphoreType.DMA
@@ -420,9 +495,13 @@
         jax.ShapeDtypeStruct((2, row_blocks * width, width), F32),
         jax.ShapeDtypeStruct(k_inv.shape, F32),
     )
-    piece = (width // bands, width)
+
+    def per_group(lead, rows, kind):
+        return [pltpu.VMEM(lead + (rows, (hi - lo) * LANES), kind) for lo, hi in spans]
+
+    band_rows = LANES // 2
     results = pl.pallas_call(
-        functools.partial(kernel, n_rows, n_cols),
+        functools.partial(kernel, n_rows, n_cols, spans),
         out_shape=tuple(pltpu.VMEM(s.shape, s.dtype) for s in shapes),
         in_specs=[hbm, hbm, hbm, hbm, hbm],
         out_specs=(vmem, vmem),
@@ -432,26 +511,26 @@
             pltpu.VMEM(panel.shape, BF16),
             pltpu.VMEM((2, width, width), BF16),
             pltpu.VMEM((n_cols, 2, part, width), BF16),
-            pltpu.VMEM((2, n_cols, n_rows, part, width), BF16),
             pltpu.VMEM((n_cols - 1, 2, width, width), BF16),
             pltpu.VMEM((n_cols, 2, width, width), BF16),
-            pltpu.VMEM((2, width, width), F32),
+            pltpu.VMEM((2, width, 2 * width), F32),
             pltpu.VMEM(k_inv.shape, F32),
             pltpu.VMEM((2, width, width), BF16),
-            pltpu.VMEM((2, share) + piece, F32),
-            pltpu.VMEM((2, bands) + piece, BF16),
-            pltpu.VMEM((n_rows, 2, share) + piece, BF16),
-            pltpu.VMEM((2, bands) + piece, BF16),
+            *per_group((n_cols, n_rows), part, BF16),
+            *per_group((share,), band_rows, F32),
+            *per_group((tiles,), band_rows, BF16),
+            *per_group((n_rows, share), band_rows, BF16),
+            *per_group((tiles,), band_rows, BF16),
             dma((4,)),
             dma((1,)),
             dma((n_cols - 1,)),
             dma((1,)),
             dma((n_cols - 1,)),
             dma((1,)),
-            dma((3 * n_cols + 2,)),
+            dma((4 * n_cols + 1,)),
             dma((1,)),
-            dma((2, share)),
-            dma((2, 2)),
+            dma((share + 2,)),
+            dma((6,)),
         ],
         compiler_params=pltpu.CompilerParams(
             collective_id=0, has_side_effects=True
@@ -487,6 +566,7 @@
         and u_inv.shape[1] == cols
         and cols // 2 == 2
         and cols % 2 == 0
+        and block_width == 2 * LANES
     ):
         return compact(ainv_anc, panel, u_inv, k_inv, structure)
     total_k = u_inv.shape[1]

time: 35.4 us -> 35.2 us (level)
  no operation moved by 1% of the time
where the time goes in v5:
time: 35.2 us; the launch traced here: 35.1 us
  Pallas kernels  34.4 us (98%)
  between operations  0.64 us (2%)
    pallas_call x1, Pallas kernels, compact(): pl.pallas_call(functools.partial(kernel, n_rows, n_cols, spans), out_shap...  33.3 us
    pallas_call x1, Pallas kernels, compact(): pl.pallas_call(place, out_shape=shapes, in_specs=[vmem, vmem], out_specs=...  1.16 us

profile of v5, /device:TPU:0, one launch (start us, length us, event | category | flops | bytes accessed | tf_op | source)
XLA Modules:
  0.0 35.1 jit_solution(11645119680830392048)
XLA Ops:
  0.6 33.3 %shard_map.68 = (f32[2,512,256]{2,1,0:T(8,128)S(1)}, f32[2,1,256,256]{3,2,1,0:T(8,128)S(1)}) custom-call(bf16[2,512,512]{2,1,0:T(8,128)(2,1)} %a_hbm.1, bf16[2,4,64,256]{3,2,1,0:T(8,128)(2,1)} %panel_hbm.1, bf16[2,4,256,256]{3,2,1,0:T(8,128)(2,1)} %u_hbm.1, f32[2,1,256,256]{3,2,1,0:T(8,128)} %k_hbm.1, s32[4,4]{1,0:T(4,128)} %table_hbm.1), custom_call_target="tpu_custom_call" | custom-call | tf_op jit(solution)/shard_map/pallas_call | solution.py:503
  33.9 1.2 %shard_map.69 = (f32[2,512,256]{2,1,0:T(8,128)}, f32[2,1,256,256]{3,2,1,0:T(8,128)}) custom-call(f32[2,512,256]{2,1,0:T(8,128)S(1)} %get-tuple-element.4.sel, f32[2,1,256,256]{3,2,1,0:T(8,128)S(1)} %get-tuple-element.5.diag), custom_call_target="tpu_custom_call" | custom-call | tf_op jit(solution)/shard_map/pallas_call | solution.py:539

commit v6 on v5

--- a/solution.py
+++ b/solution.py
@@ -315,45 +315,49 @@
                 acc[plane, :, span(group)] += value
 
     home = unit_of(row)
-    live = (jnp.full((1, LANES), table[col, row]) >= 0).astype(F32)
     named = jnp.full((1, LANES), table[col, row]) - row * row_blocks
 
     def pieces(group):
-        return [(part, 1) for part in range(share)] if group == 0 else [(0, share)]
-
-    def quad_copy(group, there, piece, source):
+        return [(0, share)] if group == 1 else [(part, 1) for part in range(share)]
+
+    def slot_of(group, part):
+        return (0, share, share + 1)[group] + part
+
+    def quad_copy(group, there, piece):
         part, count = piece
-        at = (there - first) * share + part
+        at = part if there is over else share + part
         return remote(
-            q_out[group].at[pl.ds(at, count)], q_in[group].at[source, part : part + count],
-            d_send.at[0], q_recv.at[group + share - 1 if group else part], {"prow": there},
+            q_out[group].at[at : at + count], q_in[group].at[row, part : part + count],
+            d_send.at[0], q_recv.at[slot_of(group, part)], {"prow": there},
         )
 
-    def quad(group):
-        value = join(acc[0, :, span(group)], acc[1, :, span(group)])
-        value = jnp.concatenate([x * live for x in tiles_of(value)], axis=1)
+    def quad(group, unit):
+        right = gather[group][unit].reshape(width, gather[group].shape[-1])
+        slot = peer(unit)
+        sums = [
+            acc[plane, :, span(group)] + jnp.dot(picks[slot, plane], right, preferred_element_type=F32)
+            for plane in range(2)
+        ]
+        value = join(*sums)
+        product = jnp.dot(z_t[...].reshape(2 * width, width), value.astype(BF16), preferred_element_type=F32)
+        for piece in pieces(group):
+            for half in range(2):
+                for part in range(piece[0], piece[0] + piece[1]):
+                    at = (half * share + part) * LANES
+                    block = join(product[at : at + band_rows], product[at + band_rows : at + LANES])
+                    q_out[group][half * share + part] = block.astype(BF16)
+                    if half:
+                        own[group][part] = block
+                if half:
+
+                    @pl.when(is_end)
+                    def _():
+                        quad_copy(group, mate, piece).start()
+
+                else:
+                    quad_copy(group, over, piece).start()
+
         acc[0, :, span(group)] = value
-        low = value.astype(BF16)
-        for there in (over, inner):
-            top = there - first
-            product = jnp.dot(z_t[top], low, preferred_element_type=F32)
-            for part in range(share):
-                at = part * LANES
-                block = join(product[at : at + band_rows], product[at + band_rows : at + LANES])
-                q_out[group][top * share + part] = block.astype(BF16)
-                if there is inner:
-                    own[group][part] = block
-
-            if there is over:
-                quad_copy(group, over, pieces(group)[0], row).start()
-
-        for number, piece in enumerate(pieces(group)):
-            if number > 0:
-                quad_copy(group, over, piece, row).start()
-
-            @pl.when(is_end)
-            def _():
-                quad_copy(group, mate, piece, row).start()
 
     for unit in range(n_cols):
         with scope(f"ready_g0_{unit}"):
@@ -367,22 +371,25 @@
                 for tile in range(*spans[group]):
                     at = (tile - spans[group][0]) * LANES
                     to = (tile % share) * LANES
-                    z_t[tile // share, to : to + LANES, :] = turned[at : at + LANES]
+                    part = jnp.where(over - first == tile // share, 0, 1)
+                    z_t[part, to : to + LANES, :] = turned[at : at + LANES]
         with scope(f"wpick_{unit}"):
             if unit > 0:
                 pick_copy(unit, peer(unit)).wait_recv()
-        multiply(0, unit, unit == 0)
+        if unit < n_cols - 1:
+            multiply(0, unit, unit == 0)
     with scope("quad0"):
-        quad(0)
+        quad(0, n_cols - 1)
     for group in groups[1:]:
         for i in range(n_cols):
             unit = (home + i) % n_cols
             if i > 0:
                 with scope(f"ready_g{group}_{i}"):
                     ready(group, unit)
-            multiply(group, unit, i == 0)
+            if i < n_cols - 1:
+                multiply(group, unit, i == 0)
         with scope(f"quad{group}"):
-            quad(group)
+            quad(group, unit)
 
     for pair in range(width // LANES):
         at = 2 * pair * LANES
@@ -434,7 +441,7 @@
                 with scope(f"wq{group}_{part}"):
                     arrived(
                         q_in[group].at[0 : n_rows - 1, part : part + count],
-                        q_recv.at[group + share - 1 if group else part],
+                        q_recv.at[slot_of(group, part)],
                     )
                 for at in range(part, part + count):
                     total = own[group][at]
@@ -529,7 +536,7 @@
             dma((1,)),
             dma((4 * n_cols + 1,)),
             dma((1,)),
-            dma((share + 2,)),
+            dma((2 * share + 1,)),
             dma((6,)),
         ],
         compiler_params=pltpu.CompilerParams(

time: 35.2 us -> 35 us (level)
  no operation moved by 1% of the time
where the time goes in v6:
time: 35 us; the launch traced here: 34.8 us
  Pallas kernels  34.2 us (98%)
  between operations  0.64 us (2%)
    pallas_call x1, Pallas kernels, compact(): pl.pallas_call(functools.partial(kernel, n_rows, n_cols, spans), out_shap...  33 us
    pallas_call x1, Pallas kernels, compact(): pl.pallas_call(place, out_shape=shapes, in_specs=[vmem, vmem], out_specs=...  1.16 us

profile of v6, /device:TPU:0, one launch (start us, length us, event | category | flops | bytes accessed | tf_op | source)
XLA Modules:
  0.0 34.8 jit_solution(15414940619484726099)
XLA Ops:
  0.6 33.0 %shard_map.68 = (f32[2,512,256]{2,1,0:T(8,128)S(1)}, f32[2,1,256,256]{3,2,1,0:T(8,128)S(1)}) custom-call(bf16[2,512,512]{2,1,0:T(8,128)(2,1)} %a_hbm.1, bf16[2,4,64,256]{3,2,1,0:T(8,128)(2,1)} %panel_hbm.1, bf16[2,4,256,256]{3,2,1,0:T(8,128)(2,1)} %u_hbm.1, f32[2,1,256,256]{3,2,1,0:T(8,128)} %k_hbm.1, s32[4,4]{1,0:T(4,128)} %table_hbm.1), custom_call_target="tpu_custom_call" | custom-call | tf_op jit(solution)/shard_map/pallas_call | solution.py:510
  33.6 1.2 %shard_map.69 = (f32[2,512,256]{2,1,0:T(8,128)}, f32[2,1,256,256]{3,2,1,0:T(8,128)}) custom-call(f32[2,512,256]{2,1,0:T(8,128)S(1)} %get-tuple-element.4.sel, f32[2,1,256,256]{3,2,1,0:T(8,128)S(1)} %get-tuple-element.5.diag), custom_call_target="tpu_custom_call" | custom-call | tf_op jit(solution)/shard_map/pallas_call | solution.py:546

commit v7 on v5

v7 whole, which is shorter than its diff:
```python
import functools

import jax
import jax.numpy as jnp
from jax import lax
from jax.experimental import pallas as pl
from jax.experimental.pallas import tpu as pltpu
from jax.sharding import PartitionSpec as P

BF16 = jnp.bfloat16
F32 = jnp.float32
LANES = 128
scope = jax.named_scope


def cdot(left, right, dims=(((1,), (0,)), ((), ()))):
    def single(x, y):
        return lax.dot_general(x, y, dims, preferred_element_type=F32)

    real = single(left[0], right[0]) - single(left[1], right[1])
    imag = single(left[0], right[1]) + single(left[1], right[0])
    return real, imag


def remote(src, dst, send_sem, recv_sem, where):
    return pltpu.make_async_remote_copy(
        src_ref=src,
        dst_ref=dst,
        send_sem=send_sem,
        recv_sem=recv_sem,
        device_id=where,
        device_id_type=pl.DeviceIdType.MESH,
    )


def swap(x):
    return pltpu.roll(x, x.shape[1] // 2, 1)


def low_lanes():
    return lax.broadcasted_iota(jnp.int32, (1, LANES), 1) < LANES // 2


def tiles_of(x):
    return [x[:, at : at + LANES] for at in range(0, x.shape[1], LANES)]


def join(left, right):
    sign = jnp.where(low_lanes(), -1.0, 1.0)
    return jnp.concatenate([a + swap(b) * sign for a, b in zip(tiles_of(left), tiles_of(right))], axis=1)


def cross(a, b):
    low = low_lanes()
    return jnp.where(low, a, swap(b)), jnp.where(low, swap(a), b)


def kernel(
    n_rows, n_cols, spans, a_hbm, panel_hbm, u_hbm, k_hbm, table_hbm, sel_out, diag_out,
    table, av, pv, uv, pr, pick_out, picks, acc, kv, z_t,
    gather_0, gather_1, gather_2, own_0, own_1, own_2, out_0, out_1, out_2,
    in_0, in_1, in_2, tot_0, tot_1, tot_2,
    d_send, q_recv, t_recv,
):
    gather, own = (gather_0, gather_1, gather_2), (own_0, own_1, own_2)
    q_out, q_in, tot = (out_0, out_1, out_2), (in_0, in_1, in_2), (tot_0, tot_1, tot_2)
    groups = range(len(spans))
    row = lax.axis_index("prow")
    col = lax.axis_index("pcol")
    width = u_hbm.shape[-1]
    pairs = n_cols // 2
    row_blocks = a_hbm.shape[1] // width
    col_blocks = a_hbm.shape[2] // width
    band_rows = LANES // 2
    share = q_in[0].shape[1]
    first = n_rows // 2 - 1
    mate = row + 1 - 2 * (row % 2)
    is_end = (row == 0) | (row == n_rows - 1)
    is_inner = jnp.logical_not(is_end)
    end = jnp.where(is_end, row, mate)
    inner = jnp.where(is_end, mate, row)
    over = n_rows - 1 - inner
    far = n_rows - 1 - end

    def peer(unit):
        return ((col // 2 + unit // 2) % pairs) * 2 + (col + unit) % 2

    def unit_of(slot):
        return ((slot // 2 - col // 2 + pairs) % pairs) * 2 + (slot + col) % 2

    def arrived(view, sem):
        remote(view, view, sem, sem, {"prow": mate}).wait_recv()

    def drain(view, sem):
        remote(view, view, sem, sem, {"prow": mate}).wait_send()

    def pieces(group):
        cuts = 1 if group else 2
        rows = band_rows // cuts
        return [(part, slice(cut * rows, (cut + 1) * rows)) for part in range(share) for cut in range(cuts)]

    def slot_of(group, piece):
        before = sum(len(pieces(other)) for other in range(group))
        return before + pieces(group).index(piece)

    def gathering(local_sem, p_send, p_recv, a_send, a_recv, g_send, g_recv):
        copy_p = pltpu.make_async_copy(panel_hbm, pv, local_sem.at[0])
        copy_u = pltpu.make_async_copy(u_hbm.at[:, col], uv, local_sem.at[1])
        copy_t = pltpu.make_async_copy(table_hbm, table, local_sem.at[2])
        copy_a = pltpu.make_async_copy(a_hbm, av, local_sem.at[3])
        copy_k = pltpu.make_async_copy(k_hbm, kv, local_sem.at[2])
        copy_p.start()
        copy_u.start()
        copy_t.start()
        copy_a.start()

        barrier = pltpu.get_barrier_semaphore()

        def greet(axis, there):
            pl.semaphore_signal(barrier, inc=1, device_id={axis: there}, device_id_type=pl.DeviceIdType.MESH)

        for unit in range(1, n_cols):
            greet("pcol", peer(unit))
        greet("prow", mate)
        greet("prow", jnp.where(is_end, over, far))

        @pl.when(is_inner)
        def _():
            greet("prow", over)

        def panel_copy(unit, source):
            return remote(
                pv.at[:, peer(unit)], pr.at[source], p_send.at[0], p_recv.at[unit - 1], {"pcol": peer(unit)}
            )

        def pick_copy(unit, source):
            return remote(
                pick_out.at[unit - 1], picks.at[source], a_send.at[0], a_recv.at[unit - 1], {"pcol": peer(unit)}
            )

        def base(group):
            return (group + 1) * n_cols if group else 0

        all_mate = 4 * n_cols

        def chunk_copy(group, unit, chunk, index, there):
            block = gather[group].at[unit, chunk]
            return remote(block, block, g_send.at[0], g_recv.at[index], {"prow": there})

        def scale(unit):
            slot = peer(unit)
            if unit == 0:
                left = (pv[0, col], pv[1, col])
            else:
                panel_copy(unit, slot).wait_recv()
                left = (pr[slot, 0], pr[slot, 1])
            real, imag = cdot(left, (uv[0], uv[1]))
            live = (jnp.full((1, width), table[col, slot]) >= 0).astype(F32)
            packed = []
            for a, b in zip(tiles_of(real * live), tiles_of(imag * live)):
                packed.extend(cross(a, b))
            for group in groups:
                lo, hi = spans[group]
                for tile in range(lo, hi):
                    at = (tile - lo) * LANES
                    gather[group][unit, row, :, at : at + LANES] = packed[tile].astype(BF16)

        def send_over(group, unit):
            index = base(group) + unit if group else unit + jnp.where(is_end, n_cols, 0)
            chunk_copy(group, unit, row, index, over).start()

        def send_mate(group, unit):
            chunk_copy(group, unit, row, jnp.where(is_end, all_mate, base(group) + unit), mate).start()

        def pick(unit):
            node = peer(unit)
            top = jnp.full((1, width), table[node, row]) - row * row_blocks
            side = jnp.full((1, width), table[node, col]) - col * col_blocks
            for plane in range(2):
                total = None
                for i in range(row_blocks):
                    for j in range(col_blocks):
                        keep = ((top == i) & (side == j)).astype(F32).astype(BF16)
                        block = av[plane, i * width : (i + 1) * width, j * width : (j + 1) * width] * keep
                        total = block if total is None else total + block
                if unit == 0:
                    picks[col, plane] = total
                else:
                    pick_out[unit - 1, plane] = total

        with scope("copies"):
            copy_p.wait()
            copy_u.wait()
            copy_t.wait()
        copy_k.start()
        with scope("scale0"):
            scale(0)
        with scope("barrier"):
            pl.semaphore_wait(barrier, n_cols + 2 - is_end.astype(jnp.int32))
        for unit in range(1, n_cols):
            panel_copy(unit, col).start()
        send_over(0, 0)
        send_mate(0, 0)
        with scope("scale1"):
            scale(1)
        send_over(0, 1)
        send_mate(0, 1)
        far_home = unit_of(far)
        early = jnp.where(far_home < 2, far_home, 0)
        for group in groups[1:]:
            send_over(group, early)

        @pl.when(is_end)
        def _():
            for group in groups[1:]:
                send_mate(group, early)

        @pl.when(is_inner)
        def _():
            for unit in range(2):
                for group in groups[1:]:
                    send_mate(group, unit)

        with scope("copy_a"):
            copy_a.wait()
        for unit in list(range(2, n_cols)) + [1]:
            with scope(f"pick{unit}"):
                pick(unit)
            pick_copy(unit, col).start()
        pick(0)
        late = range(2, n_cols)
        order = [(group, 0) for group in groups[1:]] + [(group, i) for group in groups[1:] for i in range(1, n_cols)]

        def relay(unit, chunk, index):
            arrived(gather[0].at[unit, chunk], g_recv.at[index])
            chunk_copy(0, unit, chunk, unit, end).start()

        def relay_both(group, unit):
            index = base(group) + unit
            arrived(gather[group].at[unit, 0:2], g_recv.at[index])
            chunk_copy(group, unit, over, index, end).start()
            chunk_copy(group, unit, far, index, end).start()

        @pl.when(is_end)
        def _():
            for unit in late:
                with scope(f"scale{unit}"):
                    scale(unit)
                send_over(0, unit)
                send_mate(0, unit)
            for group, i in order:
                unit = (far_home + i) % n_cols

                @pl.when(unit != early)
                def _():
                    send_over(group, unit)
                    send_mate(group, unit)

        @pl.when(is_inner)
        def _():
            with scope("relay_0o"):
                relay(0, over, 0)
            with scope("scale2"):
                scale(2)
            send_over(0, 2)
            send_mate(0, 2)
            with scope("relay_1o"):
                relay(1, over, 1)
            with scope("scale3"):
                scale(3)
            send_over(0, 3)
            send_mate(0, 3)
            with scope("relay_01f"):
                relay(0, far, n_cols)
                relay(1, far, n_cols + 1)
            for group, i in order:
                unit = (far_home + i) % n_cols

                @pl.when(unit != early)
                def _():
                    send_over(group, unit)

            home = unit_of(end)

            @pl.when(home >= 2)
            def _():
                for group in groups[1:]:
                    send_mate(group, home)

            for unit in late:
                with scope(f"relay_{unit}o"):
                    relay(unit, over, unit)
                with scope(f"relay_{unit}f"):
                    relay(unit, far, n_cols + unit)
            for group, i in order:
                if i == 1:
                    for unit in late:

                        @pl.when(unit != home)
                        def _():
                            send_mate(group, unit)

                with scope(f"relay_g{group}_{i}"):
                    relay_both(group, (home + i) % n_cols)
            with scope("mate"):
                arrived(picks.at[0], g_recv.at[all_mate])

        def ready(group, unit):
            @pl.when(is_end)
            def _():
                arrived(gather[group].at[unit, 0 : n_rows - 1], g_recv.at[base(group) + unit])

        def span(group):
            lo, hi = spans[group]
            return slice(lo * LANES, hi * LANES)

        def multiply(group, unit, start):
            right = gather[group][unit].reshape(width, gather[group].shape[-1])
            slot = peer(unit)
            for plane in range(2):
                value = jnp.dot(picks[slot, plane], right, preferred_element_type=F32)
                if start:
                    acc[plane, :, span(group)] = value
                else:
                    acc[plane, :, span(group)] += value

        home = unit_of(row)
        named = jnp.full((1, LANES), table[col, row]) - row * row_blocks

        def quad_copy(group, there, piece):
            part, rows = piece
            at = part if there is over else share + part
            return remote(
                q_out[group].at[at, rows], q_in[group].at[row, part, rows],
                d_send.at[0], q_recv.at[slot_of(group, piece)], {"prow": there},
            )

        def quad(group, unit):
            right = gather[group][unit].reshape(width, gather[group].shape[-1])
            slot = peer(unit)
            sums = [
                acc[plane, :, span(group)] + jnp.dot(picks[slot, plane], right, preferred_element_type=F32)
                for plane in range(2)
            ]
            value = join(*sums)
            product = jnp.dot(z_t[...].reshape(2 * width, width), value.astype(BF16), preferred_element_type=F32)
            for piece in pieces(group):
                for half in range(2):
                    part, rows = piece
                    at = (half * share + part) * LANES
                    upper = product[at + rows.start : at + rows.stop]
                    lower = product[at + band_rows + rows.start : at + band_rows + rows.stop]
                    block = join(upper, lower)
                    q_out[group][half * share + part, rows] = block.astype(BF16)
                    if half:
                        own[group][part, rows] = block
                    if half:

                        @pl.when(is_end)
                        def _():
                            quad_copy(group, mate, piece).start()

                    else:
                        quad_copy(group, over, piece).start()

            acc[0, :, span(group)] = value

        for unit in range(n_cols):
            with scope(f"ready_g0_{unit}"):
                ready(0, unit)
            if unit == n_cols - 1:
                with scope("ready_home"):
                    for group in groups[1:]:
                        ready(group, home)
                for group in groups:
                    turned = gather[group][home].reshape(width, gather[group].shape[-1]).T
                    for tile in range(*spans[group]):
                        at = (tile - spans[group][0]) * LANES
                        to = (tile % share) * LANES
                        part = jnp.where(over - first == tile // share, 0, 1)
                        z_t[part, to : to + LANES, :] = turned[at : at + LANES]
            with scope(f"wpick_{unit}"):
                if unit > 0:
                    pick_copy(unit, peer(unit)).wait_recv()
            if unit < n_cols - 1:
                multiply(0, unit, unit == 0)
        with scope("quad0"):
            quad(0, n_cols - 1)
        for group in groups[1:]:
            for i in range(n_cols):
                unit = (home + i) % n_cols
                if i > 0:
                    with scope(f"ready_g{group}_{i}"):
                        ready(group, unit)
                if i < n_cols - 1:
                    multiply(group, unit, i == 0)
            with scope(f"quad{group}"):
                quad(group, unit)

        for pair in range(width // LANES):
            at = 2 * pair * LANES
            planes = cross(acc[0, :, at : at + LANES], acc[0, :, at + LANES : at + 2 * LANES])
            columns = slice(pair * LANES, (pair + 1) * LANES)
            for i in range(row_blocks):
                keep = -(named == i).astype(F32)
                for plane in range(2):
                    sel_out[plane, i * width : (i + 1) * width, columns] = planes[plane] * keep
        copy_k.wait()
        drain(pr.at[0 : n_cols - 1], p_send.at[0])
        drain(pick_out, a_send.at[0])

        @pl.when(is_inner)
        def _():
            drain(picks, g_send.at[0])

        @pl.when(is_end)
        def _():
            drain(picks.at[0:2], g_send.at[0])
            drain(picks.at[0], d_send.at[0])

    dma = pltpu.SemaphoreType.DMA
    pl.run_scoped(
        gathering, dma((4,)), dma((1,)), dma((n_cols - 1,)), dma((1,)), dma((n_cols - 1,)), dma((1,)), dma((4 * n_cols + 1,))
    )

    def total_copy(group, piece, there):
        part, rows = piece
        block = tot[group].at[(row - first) * share + part, rows]
        return remote(block, block, d_send.at[0], t_recv.at[group * 2 + row - first], {"prow": there})

    where_tile = {tile: group for group in groups for tile in range(*spans[group])}

    def tile_of(tile, band):
        group = where_tile[tile]
        at = (tile - spans[group][0]) * LANES
        return tot[group][band, :, at : at + LANES].astype(F32)

    def finish(pair, owner):
        columns = slice(pair * LANES, (pair + 1) * LANES)
        for part in range(share):
            band = owner * share + part
            rows = pl.ds(pl.multiple_of(band * band_rows, band_rows), band_rows)
            planes = cross(tile_of(2 * pair, band), tile_of(2 * pair + 1, band))
            for plane in range(2):
                diag_out[plane, 0, rows, columns] = kv[plane, 0, rows, columns] + planes[plane]

    @pl.when(is_inner)
    def _():
        for group in groups:
            for piece in pieces(group):
                part, rows = piece
                with scope(f"wq{slot_of(group, piece)}"):
                    arrived(q_in[group].at[0 : n_rows - 1, part, rows], q_recv.at[slot_of(group, piece)])
                total = own[group][part, rows]
                for source in (over, end, far):
                    total = total + q_in[group][source, part, rows].astype(F32)
                tot[group][(row - first) * share + part, rows] = total.astype(BF16)
                total_copy(group, piece, far).start()
                total_copy(group, piece, end).start()
        for group in groups:
            for part in range(share):
                total_copy(group, (part, slice(0, band_rows)), over).start()
        for pair in range(width // LANES):
            finish(pair, row - first)

    def total_wait(group, owner):
        arrived(tot[group].at[0:share], t_recv.at[group * 2 + owner])

    @pl.when(is_end)
    def _():
        for group in groups:
            for there in (inner, over):
                with scope(f"wt{group}"):
                    total_wait(group, there - first)
                if group != 1:
                    finish(1 if group else 0, there - first)

    @pl.when(is_inner)
    def _():
        for group in groups:
            with scope(f"wt{group}"):
                total_wait(group, over - first)
        for pair in range(width // LANES):
            finish(pair, over - first)
        drain(picks.at[0:2], d_send.at[0])


def place(sel, diag, sel_out, diag_out, out_sem):
    copies = [
        pltpu.make_async_copy(sel, sel_out, out_sem.at[0]),
        pltpu.make_async_copy(diag, diag_out, out_sem.at[1]),
    ]
    for copy in copies:
        copy.start()
    for copy in copies:
        copy.wait()


def compact(ainv_anc, panel, u_inv, k_inv, structure):
    n_rows, n_cols = lax.axis_size("prow"), lax.axis_size("pcol")
    width, part = u_inv.shape[-1], panel.shape[2]
    row_blocks = ainv_anc.shape[1] // width
    tiles = 2 * width // LANES
    share = tiles // 2
    spans = ((0, share), (share, share + share // 2), (share + share // 2, tiles))
    hbm = pl.BlockSpec(memory_space=pltpu.HBM)
    vmem = pl.BlockSpec(memory_space=pltpu.VMEM)
    dma = pltpu.SemaphoreType.DMA
    shapes = (
        jax.ShapeDtypeStruct((2, row_blocks * width, width), F32),
        jax.ShapeDtypeStruct(k_inv.shape, F32),
    )

    def per_group(lead, rows, kind):
        return [pltpu.VMEM(lead + (rows, (hi - lo) * LANES), kind) for lo, hi in spans]

    band_rows = LANES // 2
    results = pl.pallas_call(
        functools.partial(kernel, n_rows, n_cols, spans),
        out_shape=tuple(pltpu.VMEM(s.shape, s.dtype) for s in shapes),
        in_specs=[hbm, hbm, hbm, hbm, hbm],
        out_specs=(vmem, vmem),
        scratch_shapes=[
            pltpu.SMEM(structure.shape, jnp.int32),
            pltpu.VMEM(ainv_anc.shape, BF16),
            pltpu.VMEM(panel.shape, BF16),
            pltpu.VMEM((2, width, width), BF16),
            pltpu.VMEM((n_cols, 2, part, width), BF16),
            pltpu.VMEM((n_cols - 1, 2, width, width), BF16),
            pltpu.VMEM((n_cols, 2, width, width), BF16),
            pltpu.VMEM((2, width, 2 * width), F32),
            pltpu.VMEM(k_inv.shape, F32),
            pltpu.VMEM((2, width, width), BF16),
            *per_group((n_cols, n_rows), part, BF16),
            *per_group((share,), band_rows, F32),
            *per_group((tiles,), band_rows, BF16),
            *per_group((n_rows, share), band_rows, BF16),
            *per_group((tiles,), band_rows, BF16),
            dma((1,)),
            dma((4 * share,)),
            dma((6,)),
        ],
        compiler_params=pltpu.CompilerParams(
            collective_id=0, has_side_effects=True
        ),
    )(ainv_anc, panel, u_inv, k_inv, structure)
    return pl.pallas_call(
        place,
        out_shape=shapes,
        in_specs=[vmem, vmem],
        out_specs=(hbm, hbm),
        scratch_shapes=[dma((2,))],
    )(*[pltpu.with_memory_space_constraint(x, pltpu.VMEM) for x in results])


def complex_quad(z_part, s_part):
    highest = lax.Precision.HIGHEST

    def single(left, right):
        return jnp.einsum("kra,rkb->kab", left, right, precision=highest)

    real = single(z_part[0], s_part[0]) - single(z_part[1], s_part[1])
    imag = single(z_part[0], s_part[1]) + single(z_part[1], s_part[0])
    return jnp.stack([real, imag])


def local(ainv_anc, panel, u_inv, k_inv, structure):
    block_width = u_inv.shape[-1]
    cols = lax.axis_size("pcol")
    if (
        structure.shape[1] == cols
        and lax.axis_size("prow") == cols
        and ainv_anc.shape[1] == ainv_anc.shape[2]
        and u_inv.shape[1] == cols
        and cols // 2 == 2
        and cols % 2 == 0
        and block_width == 2 * LANES
    ):
        return compact(ainv_anc, panel, u_inv, k_inv, structure)
    total_k = u_inv.shape[1]
    own_k = k_inv.shape[1]
    n_cols = lax.axis_size("pcol")
    row_here = lax.axis_index("prow")
    col_here = lax.axis_index("pcol")
    row_blocks = ainv_anc.shape[1] // block_width
    group_blocks = ainv_anc.shape[2] // block_width
    group_slots = structure.shape[1] // n_cols
    rows_all = row_blocks * block_width
    col_struct = lax.dynamic_slice_in_dim(structure, col_here * group_slots, group_slots, 1)
    slot_live = col_struct >= 0
    slot_pos = col_struct - col_here * group_blocks
    first_block = row_here * row_blocks
    target = first_block + jnp.arange(row_blocks, dtype=jnp.int32)
    rows_in = lax.all_gather(panel, "prow", axis=2, tiled=True)

    def single(left, right):
        return jnp.einsum("knb,kbc->knc", left, right, preferred_element_type=jnp.float32)

    real = single(rows_in[0], u_inv[0]) - single(rows_in[1], u_inv[1])
    imag = single(rows_in[0], u_inv[1]) + single(rows_in[1], u_inv[0])
    placed = jnp.stack([real, imag]).astype(jnp.bfloat16)
    placed = placed.reshape(2, total_k, group_slots, block_width, block_width)
    placed = jnp.where(slot_live[None, :, :, None, None], placed, jnp.zeros((), jnp.bfloat16))
    block_ids = jnp.arange(group_blocks, dtype=jnp.int32)
    pick_table = (slot_pos[:, :, None] == block_ids[None, None, :]).astype(jnp.bfloat16)
    ainv_blocks = ainv_anc.reshape(2, rows_all, group_blocks, block_width)

    def one_node(items):
        table_k, rows_k = items
        picked = jnp.einsum(
            "sg,cigw->cisw", table_k, ainv_blocks, preferred_element_type=jnp.float32
        )
        picked = picked.astype(jnp.bfloat16).reshape(2, rows_all, group_slots * block_width)
        right = rows_k.reshape(2, group_slots * block_width, block_width)
        real = jnp.dot(picked[0], right[0], preferred_element_type=jnp.float32) - jnp.dot(
            picked[1], right[1], preferred_element_type=jnp.float32
        )
        imag = jnp.dot(picked[0], right[1], preferred_element_type=jnp.float32) + jnp.dot(
            picked[1], right[0], preferred_element_type=jnp.float32
        )
        return jnp.stack([real, imag])

    per_node = lax.map(one_node, (pick_table, jnp.moveaxis(placed, 1, 0)))
    partial_value = jnp.transpose(per_node, (1, 2, 0, 3))
    row_table = (col_struct[:, None, :] == target[None, :, None]).astype(jnp.bfloat16)
    z_rows = jnp.einsum("kts,ckswb->cktwb", row_table, placed, preferred_element_type=jnp.float32)
    z_rows = z_rows.astype(jnp.bfloat16).reshape(2, total_k, rows_all, block_width)
    summed = lax.psum_scatter(
        partial_value.reshape(2, rows_all, total_k * block_width),
        "pcol",
        scatter_dimension=2,
        tiled=True,
    )
    own_struct = lax.dynamic_slice_in_dim(structure, col_here * own_k, own_k, 0)
    member = jnp.any(own_struct[:, :, None] == target[None, None, :], axis=1)
    selected = -summed.reshape(2, row_blocks, block_width, own_k, block_width)
    selected = jnp.where(member.T[None, :, None, :, None], selected, 0.0)
    sel_inv = selected.reshape(2, rows_all, own_k * block_width)
    received = lax.all_to_all(z_rows, "pcol", split_axis=1, concat_axis=1, tiled=True)
    z_own = (
        received.astype(jnp.float32).reshape(2, n_cols, own_k, rows_all, block_width).sum(axis=1)
    )
    quad_term = complex_quad(z_own, selected.reshape(2, rows_all, own_k, block_width))
    total_sum = lax.psum(quad_term, "prow")
    diag_inv = k_inv - total_sum
    return (sel_inv, diag_inv)


def solution(mesh):
    placed = (
        P(None, ("pole", "prow"), "pcol"),
        P(None, "pole", ("pcol", "prow"), None),
        P(None, "pole", None, None),
        P(None, ("pole", "pcol"), None, None),
        P(),
    )
    return jax.shard_map(
        local,
        mesh=mesh,
        in_specs=placed,
        out_specs=(P(None, ("pole", "prow"), "pcol"), P(None, ("pole", "pcol"), None, None)),
        check_vma=False,
    )
```

time: 35.2 us -> 34.7 us (0.986)
  Pallas kernels: 34.4 us -> 33.9 us
    pallas_call x1, Pallas kernels: 33.3 us -> 32.7 us  [compact(): pl.pallas_call(functools.partial(kernel, n_rows, n_cols, spans), out_shap...]
where the time goes in v7:
time: 34.7 us; the launch traced here: 34.5 us
  Pallas kernels  33.9 us (98%)
  between operations  0.64 us (2%)
    pallas_call x1, Pallas kernels, compact(): pl.pallas_call(functools.partial(kernel, n_rows, n_cols, spans), out_shap...  32.7 us
    pallas_call x1, Pallas kernels, compact(): pl.pallas_call(place, out_shape=shapes, in_specs=[vmem, vmem], out_specs=...  1.16 us

profile of v7, /device:TPU:0, one launch (start us, length us, event | category | flops | bytes accessed | tf_op | source)
XLA Modules:
  0.0 34.5 jit_solution(18261637973993908502)
XLA Ops:
  0.6 32.7 %shard_map.68 = (f32[2,512,256]{2,1,0:T(8,128)S(1)}, f32[2,1,256,256]{3,2,1,0:T(8,128)S(1)}) custom-call(bf16[2,512,512]{2,1,0:T(8,128)(2,1)} %a_hbm.1, bf16[2,4,64,256]{3,2,1,0:T(8,128)(2,1)} %panel_hbm.1, bf16[2,4,256,256]{3,2,1,0:T(8,128)(2,1)} %u_hbm.1, f32[2,1,256,256]{3,2,1,0:T(8,128)} %k_hbm.1, s32[4,4]{1,0:T(4,128)} %table_hbm.1), custom_call_target="tpu_custom_call" | custom-call | tf_op jit(solution)/shard_map/pallas_call | solution.py:518
  33.4 1.2 %shard_map.69 = (f32[2,512,256]{2,1,0:T(8,128)}, f32[2,1,256,256]{3,2,1,0:T(8,128)}) custom-call(f32[2,512,256]{2,1,0:T(8,128)S(1)} %get-tuple-element.4.sel, f32[2,1,256,256]{3,2,1,0:T(8,128)S(1)} %get-tuple-element.5.diag), custom_call_target="tpu_custom_call" | custom-call | tf_op jit(solution)/shard_map/pallas_call | solution.py:547

commit v8 on v7

--- a/solution.py
+++ b/solution.py
@@ -59,7 +59,7 @@
     n_rows, n_cols, spans, a_hbm, panel_hbm, u_hbm, k_hbm, table_hbm, sel_out, diag_out,
     table, av, pv, uv, pr, pick_out, picks, acc, kv, z_t,
     gather_0, gather_1, gather_2, own_0, own_1, own_2, out_0, out_1, out_2,
-    in_0, in_1, in_2, tot_0, tot_1, tot_2,
+    in_0, in_1, in_2, tot_0, tot_1, tot_2, some,
     d_send, q_recv, t_recv,
 ):
     gather, own = (gather_0, gather_1, gather_2), (own_0, own_1, own_2)
@@ -99,6 +99,9 @@
         rows = band_rows // cuts
         return [(part, slice(cut * rows, (cut + 1) * rows)) for part in range(share) for cut in range(cuts)]
 
+    last = len(spans) - 1
+    slots = sum(len(pieces(group)) for group in groups)
+
     def slot_of(group, piece):
         before = sum(len(pieces(other)) for other in range(group))
         return before + pieces(group).index(piece)
@@ -188,17 +191,30 @@
                 else:
                     pick_out[unit - 1, plane] = total
 
+        def meet():
+            with scope("barrier"):
+                pl.semaphore_wait(barrier, n_cols + 2 - is_end.astype(jnp.int32))
+            for unit in range(1, n_cols):
+                panel_copy(unit, col).start()
+
+        with scope("copy_p"):
+            copy_p.wait()
+
+        @pl.when(is_end)
+        def _():
+            meet()
+
         with scope("copies"):
-            copy_p.wait()
             copy_u.wait()
             copy_t.wait()
         copy_k.start()
         with scope("scale0"):
             scale(0)
-        with scope("barrier"):
-            pl.semaphore_wait(barrier, n_cols + 2 - is_end.astype(jnp.int32))
-        for unit in range(1, n_cols):
-            panel_copy(unit, col).start()
+
+        @pl.when(is_inner)
+        def _():
+            meet()
+
         send_over(0, 0)
         send_mate(0, 0)
         with scope("scale1"):
@@ -330,9 +346,12 @@
         def quad_copy(group, there, piece):
             part, rows = piece
             at = part if there is over else share + part
+            slot = slot_of(group, piece)
+            if group == last and there is over:
+                slot = jnp.where(is_end, slots + part, slot)
             return remote(
                 q_out[group].at[at, rows], q_in[group].at[row, part, rows],
-                d_send.at[0], q_recv.at[slot_of(group, piece)], {"prow": there},
+                d_send.at[0], q_recv.at[slot], {"prow": there},
             )
 
         def quad(group, unit):
@@ -344,24 +363,26 @@
             ]
             value = join(*sums)
             product = jnp.dot(z_t[...].reshape(2 * width, width), value.astype(BF16), preferred_element_type=F32)
-            for piece in pieces(group):
-                for half in range(2):
-                    part, rows = piece
-                    at = (half * share + part) * LANES
-                    upper = product[at + rows.start : at + rows.stop]
-                    lower = product[at + band_rows + rows.start : at + band_rows + rows.stop]
-                    block = join(upper, lower)
-                    q_out[group][half * share + part, rows] = block.astype(BF16)
-                    if half:
-                        own[group][part, rows] = block
-                    if half:
-
-                        @pl.when(is_end)
-                        def _():
-                            quad_copy(group, mate, piece).start()
-
-                    else:
-                        quad_copy(group, over, piece).start()
+            turns = [(piece, half) for piece in pieces(group) for half in range(2)]
+            if group == last:
+                turns = [(piece, half) for piece in pieces(group) for half in (1, 0)]
+            for piece, half in turns:
+                part, rows = piece
+                at = (half * share + part) * LANES
+                upper = product[at + rows.start : at + rows.stop]
+                lower = product[at + band_rows + rows.start : at + band_rows + rows.stop]
+                block = join(upper, lower)
+                q_out[group][half * share + part, rows] = block.astype(BF16)
+                if half:
+                    own[group][part, rows] = block
+                if half:
+
+                    @pl.when(is_end)
+                    def _():
+                        quad_copy(group, mate, piece).start()
+
+                else:
+                    quad_copy(group, over, piece).start()
 
             acc[0, :, span(group)] = value
 
@@ -446,7 +467,7 @@
 
     @pl.when(is_inner)
     def _():
-        for group in groups:
+        for group in groups[:last]:
             for piece in pieces(group):
                 part, rows = piece
                 with scope(f"wq{slot_of(group, piece)}"):
@@ -457,6 +478,24 @@
                 tot[group][(row - first) * share + part, rows] = total.astype(BF16)
                 total_copy(group, piece, far).start()
                 total_copy(group, piece, end).start()
+        for piece in pieces(last):
+            part, rows = piece
+            slot = slot_of(last, piece)
+            with scope(f"wq{slot}"):
+                arrived(q_in[last].at[0:2, part, rows], q_recv.at[slot])
+            total = own[last][part] + q_in[last][over, part].astype(F32) + q_in[last][end, part].astype(F32)
+            some[part] = total.astype(BF16)
+            band = (row - first) * share + part
+            remote(
+                some.at[part], tot[last].at[band], d_send.at[0], t_recv.at[2 * last + row - first], {"prow": far}
+            ).start()
+        for piece in pieces(last):
+            part, rows = piece
+            with scope(f"wf{part}"):
+                arrived(q_in[last].at[0, part, rows], q_recv.at[slots + part])
+            total = some[part].astype(F32) + q_in[last][far, part].astype(F32)
+            tot[last][(row - first) * share + part] = total.astype(BF16)
+            total_copy(last, piece, end).start()
         for group in groups:
             for part in range(share):
                 total_copy(group, (part, slice(0, band_rows)), over).start()
@@ -472,6 +511,11 @@
             for there in (inner, over):
                 with scope(f"wt{group}"):
                     total_wait(group, there - first)
+                if group == last and there is over:
+                    for part in range(share):
+                        band = (over - first) * share + part
+                        total = tot[last][band].astype(F32) + q_out[last][part].astype(F32)
+                        tot[last][band] = total.astype(BF16)
                 if group != 1:
                     finish(1 if group else 0, there - first)
 
@@ -536,8 +580,9 @@
             *per_group((tiles,), band_rows, BF16),
             *per_group((n_rows, share), band_rows, BF16),
             *per_group((tiles,), band_rows, BF16),
+            pltpu.VMEM((share, band_rows, LANES), BF16),
             dma((1,)),
-            dma((4 * share,)),
+            dma((5 * share,)),
             dma((6,)),
         ],
         compiler_params=pltpu.CompilerParams(

time: 34.7 us -> 34.5 us (level)
  no operation moved by 1% of the time
where the time goes in v8:
time: 34.5 us; the launch traced here: 34.3 us
  Pallas kernels  33.7 us (98%)
  between operations  0.64 us (2%)
    pallas_call x1, Pallas kernels, compact(): pl.pallas_call(functools.partial(kernel, n_rows, n_cols, spans), out_shap...  32.5 us
    pallas_call x1, Pallas kernels, compact(): pl.pallas_call(place, out_shape=shapes, in_specs=[vmem, vmem], out_specs=...  1.16 us

profile of v8, /device:TPU:0, one launch (start us, length us, event | category | flops | bytes accessed | tf_op | source)
XLA Modules:
  0.0 34.3 jit_solution(13574984760904255069)
XLA Ops:
  0.6 32.5 %shard_map.68 = (f32[2,512,256]{2,1,0:T(8,128)S(1)}, f32[2,1,256,256]{3,2,1,0:T(8,128)S(1)}) custom-call(bf16[2,512,512]{2,1,0:T(8,128)(2,1)} %a_hbm.1, bf16[2,4,64,256]{3,2,1,0:T(8,128)(2,1)} %panel_hbm.1, bf16[2,4,256,256]{3,2,1,0:T(8,128)(2,1)} %u_hbm.1, f32[2,1,256,256]{3,2,1,0:T(8,128)} %k_hbm.1, s32[4,4]{1,0:T(4,128)} %table_hbm.1), custom_call_target="tpu_custom_call" | custom-call | tf_op jit(solution)/shard_map/pallas_call | solution.py:562
  33.1 1.2 %shard_map.69 = (f32[2,512,256]{2,1,0:T(8,128)}, f32[2,1,256,256]{3,2,1,0:T(8,128)}) custom-call(f32[2,512,256]{2,1,0:T(8,128)S(1)} %get-tuple-element.4.sel, f32[2,1,256,256]{3,2,1,0:T(8,128)S(1)} %get-tuple-element.5.diag), custom_call_target="tpu_custom_call" | custom-call | tf_op jit(solution)/shard_map/pallas_call | solution.py:592

commit v9 on v7

v9 whole, which is shorter than its diff:
```python
import functools

import jax
import jax.numpy as jnp
from jax import lax
from jax.experimental import pallas as pl
from jax.experimental.pallas import tpu as pltpu
from jax.sharding import PartitionSpec as P

BF16 = jnp.bfloat16
F32 = jnp.float32
LANES = 128
scope = jax.named_scope


def cdot(left, right, dims=(((1,), (0,)), ((), ()))):
    def single(x, y):
        return lax.dot_general(x, y, dims, preferred_element_type=F32)

    real = single(left[0], right[0]) - single(left[1], right[1])
    imag = single(left[0], right[1]) + single(left[1], right[0])
    return real, imag


def remote(src, dst, send_sem, recv_sem, where):
    return pltpu.make_async_remote_copy(
        src_ref=src,
        dst_ref=dst,
        send_sem=send_sem,
        recv_sem=recv_sem,
        device_id=where,
        device_id_type=pl.DeviceIdType.MESH,
    )


def swap(x):
    return pltpu.roll(x, x.shape[1] // 2, 1)


def low_lanes():
    return lax.broadcasted_iota(jnp.int32, (1, LANES), 1) < LANES // 2


def tiles_of(x):
    return [x[:, at : at + LANES] for at in range(0, x.shape[1], LANES)]


def join(left, right):
    sign = jnp.where(low_lanes(), -1.0, 1.0)
    return jnp.concatenate([a + swap(b) * sign for a, b in zip(tiles_of(left), tiles_of(right))], axis=1)


def cross(a, b):
    low = low_lanes()
    return jnp.where(low, a, swap(b)), jnp.where(low, swap(a), b)


def kernel(
    n_rows, n_cols, spans, a_hbm, panel_hbm, u_hbm, k_hbm, table_hbm, sel_out, diag_out,
    table, av, pv, uv, pr, pick_out, picks, acc, kv, z_t,
    gather_0, gather_1, gather_2, own_0, own_1, own_2, out_0, out_1, out_2,
    in_0, in_1, in_2, tot_0, tot_1, tot_2, some,
    d_send, t_recv,
):
    gather, own = (gather_0, gather_1, gather_2), (own_0, own_1, own_2)
    q_out, q_in, tot = (out_0, out_1, out_2), (in_0, in_1, in_2), (tot_0, tot_1, tot_2)
    groups = range(len(spans))
    row = lax.axis_index("prow")
    col = lax.axis_index("pcol")
    width = u_hbm.shape[-1]
    pairs = n_cols // 2
    row_blocks = a_hbm.shape[1] // width
    col_blocks = a_hbm.shape[2] // width
    band_rows = LANES // 2
    share = q_in[0].shape[1]
    first = n_rows // 2 - 1
    mate = row + 1 - 2 * (row % 2)
    is_end = (row == 0) | (row == n_rows - 1)
    is_inner = jnp.logical_not(is_end)
    end = jnp.where(is_end, row, mate)
    inner = jnp.where(is_end, mate, row)
    over = n_rows - 1 - inner
    far = n_rows - 1 - end

    def peer(unit):
        return ((col // 2 + unit // 2) % pairs) * 2 + (col + unit) % 2

    def unit_of(slot):
        return ((slot // 2 - col // 2 + pairs) % pairs) * 2 + (slot + col) % 2

    def arrived(view, sem):
        remote(view, view, sem, sem, {"prow": mate}).wait_recv()

    def drain(view, sem):
        remote(view, view, sem, sem, {"prow": mate}).wait_send()

    def pieces(group):
        cuts = 1 if group else 2
        rows = band_rows // cuts
        return [(part, slice(cut * rows, (cut + 1) * rows)) for part in range(share) for cut in range(cuts)]

    last = len(spans) - 1
    slots = sum(len(pieces(group)) for group in groups)

    def slot_of(group, piece):
        before = sum(len(pieces(other)) for other in range(group))
        return before + pieces(group).index(piece)

    def total_copy(group, piece, there):
        part, rows = piece
        block = tot[group].at[(row - first) * share + part, rows]
        return remote(block, block, d_send.at[0], t_recv.at[group * 2 + row - first], {"prow": there})

    where_tile = {tile: group for group in groups for tile in range(*spans[group])}

    def tile_of(tile, band):
        group = where_tile[tile]
        at = (tile - spans[group][0]) * LANES
        return tot[group][band, :, at : at + LANES].astype(F32)

    def finish(pair, owner):
        columns = slice(pair * LANES, (pair + 1) * LANES)
        for part in range(share):
            band = owner * share + part
            rows = pl.ds(pl.multiple_of(band * band_rows, band_rows), band_rows)
            planes = cross(tile_of(2 * pair, band), tile_of(2 * pair + 1, band))
            for plane in range(2):
                diag_out[plane, 0, rows, columns] = kv[plane, 0, rows, columns] + planes[plane]

    dma = pltpu.SemaphoreType.DMA

    def adding(q_recv):
        def gathering(local_sem, p_send, p_recv, a_send, a_recv, g_send, g_recv):
            copy_p = pltpu.make_async_copy(panel_hbm, pv, local_sem.at[0])
            copy_u = pltpu.make_async_copy(u_hbm.at[:, col], uv, local_sem.at[1])
            copy_t = pltpu.make_async_copy(table_hbm, table, local_sem.at[2])
            copy_a = pltpu.make_async_copy(a_hbm, av, local_sem.at[3])
            copy_k = pltpu.make_async_copy(k_hbm, kv, local_sem.at[2])
            copy_p.start()
            copy_u.start()
            copy_t.start()
            copy_a.start()

            barrier = pltpu.get_barrier_semaphore()

            def greet(axis, there):
                pl.semaphore_signal(barrier, inc=1, device_id={axis: there}, device_id_type=pl.DeviceIdType.MESH)

            for unit in range(1, n_cols):
                greet("pcol", peer(unit))
            greet("prow", mate)
            greet("prow", jnp.where(is_end, over, far))

            @pl.when(is_inner)
            def _():
                greet("prow", over)

            def panel_copy(unit, source):
                return remote(
                    pv.at[:, peer(unit)], pr.at[source], p_send.at[0], p_recv.at[unit - 1], {"pcol": peer(unit)}
                )

            def pick_copy(unit, source):
                return remote(
                    pick_out.at[unit - 1], picks.at[source], a_send.at[0], a_recv.at[unit - 1], {"pcol": peer(unit)}
                )

            def base(group):
                return (group + 1) * n_cols if group else 0

            all_mate = 4 * n_cols

            def chunk_copy(group, unit, chunk, index, there):
                block = gather[group].at[unit, chunk]
                return remote(block, block, g_send.at[0], g_recv.at[index], {"prow": there})

            def scale(unit):
                slot = peer(unit)
                if unit == 0:
                    left = (pv[0, col], pv[1, col])
                else:
                    panel_copy(unit, slot).wait_recv()
                    left = (pr[slot, 0], pr[slot, 1])
                real, imag = cdot(left, (uv[0], uv[1]))
                live = (jnp.full((1, width), table[col, slot]) >= 0).astype(F32)
                packed = []
                for a, b in zip(tiles_of(real * live), tiles_of(imag * live)):
                    packed.extend(cross(a, b))
                for group in groups:
                    lo, hi = spans[group]
                    for tile in range(lo, hi):
                        at = (tile - lo) * LANES
                        gather[group][unit, row, :, at : at + LANES] = packed[tile].astype(BF16)

            def send_over(group, unit):
                index = base(group) + unit if group else unit + jnp.where(is_end, n_cols, 0)
                chunk_copy(group, unit, row, index, over).start()

            def send_mate(group, unit):
                chunk_copy(group, unit, row, jnp.where(is_end, all_mate, base(group) + unit), mate).start()

            def pick(unit):
                node = peer(unit)
                top = jnp.full((1, width), table[node, row]) - row * row_blocks
                side = jnp.full((1, width), table[node, col]) - col * col_blocks
                for plane in range(2):
                    total = None
                    for i in range(row_blocks):
                        for j in range(col_blocks):
                            keep = ((top == i) & (side == j)).astype(F32).astype(BF16)
                            block = av[plane, i * width : (i + 1) * width, j * width : (j + 1) * width] * keep
                            total = block if total is None else total + block
                    if unit == 0:
                        picks[col, plane] = total
                    else:
                        pick_out[unit - 1, plane] = total

            def meet():
                with scope("barrier"):
                    pl.semaphore_wait(barrier, n_cols + 2 - is_end.astype(jnp.int32))
                for unit in range(1, n_cols):
                    panel_copy(unit, col).start()

            with scope("copy_p"):
                copy_p.wait()

            @pl.when(is_end)
            def _():
                meet()

            with scope("copies"):
                copy_u.wait()
                copy_t.wait()
            copy_k.start()
            with scope("scale0"):
                scale(0)

            @pl.when(is_inner)
            def _():
                meet()

            send_over(0, 0)
            send_mate(0, 0)
            with scope("scale1"):
                scale(1)
            send_over(0, 1)
            send_mate(0, 1)
            far_home = unit_of(far)
            early = jnp.where(far_home < 2, far_home, 0)
            for group in groups[1:]:
                send_over(group, early)

            @pl.when(is_end)
            def _():
                for group in groups[1:]:
                    send_mate(group, early)

            @pl.when(is_inner)
            def _():
                for unit in range(2):
                    for group in groups[1:]:
                        send_mate(group, unit)

            with scope("copy_a"):
                copy_a.wait()
            for unit in list(range(2, n_cols)) + [1]:
                with scope(f"pick{unit}"):
                    pick(unit)
                pick_copy(unit, col).start()
            pick(0)
            late = range(2, n_cols)
            order = [(group, 0) for group in groups[1:]] + [(group, i) for group in groups[1:] for i in range(1, n_cols)]

            def relay(unit, chunk, index):
                arrived(gather[0].at[unit, chunk], g_recv.at[index])
                chunk_copy(0, unit, chunk, unit, end).start()

            def relay_both(group, unit):
                index = base(group) + unit
                arrived(gather[group].at[unit, 0:2], g_recv.at[index])
                chunk_copy(group, unit, over, index, end).start()
                chunk_copy(group, unit, far, index, end).start()

            @pl.when(is_end)
            def _():
                for unit in late:
                    with scope(f"scale{unit}"):
                        scale(unit)
                    send_over(0, unit)
                    send_mate(0, unit)
                for group, i in order:
                    unit = (far_home + i) % n_cols

                    @pl.when(unit != early)
                    def _():
                        send_over(group, unit)
                        send_mate(group, unit)

            @pl.when(is_inner)
            def _():
                with scope("relay_0o"):
                    relay(0, over, 0)
                with scope("scale2"):
                    scale(2)
                send_over(0, 2)
                send_mate(0, 2)
                with scope("relay_1o"):
                    relay(1, over, 1)
                with scope("scale3"):
                    scale(3)
                send_over(0, 3)
                send_mate(0, 3)
                with scope("relay_01f"):
                    relay(0, far, n_cols)
                    relay(1, far, n_cols + 1)
                for group, i in order:
                    unit = (far_home + i) % n_cols

                    @pl.when(unit != early)
                    def _():
                        send_over(group, unit)

                home = unit_of(end)

                @pl.when(home >= 2)
                def _():
                    for group in groups[1:]:
                        send_mate(group, home)

                for unit in late:
                    with scope(f"relay_{unit}o"):
                        relay(unit, over, unit)
                    with scope(f"relay_{unit}f"):
                        relay(unit, far, n_cols + unit)
                for group, i in order:
                    if i == 1:
                        for unit in late:

                            @pl.when(unit != home)
                            def _():
                                send_mate(group, unit)

                    with scope(f"relay_g{group}_{i}"):
                        relay_both(group, (home + i) % n_cols)
                with scope("mate"):
                    arrived(picks.at[0], g_recv.at[all_mate])

            def ready(group, unit):
                @pl.when(is_end)
                def _():
                    arrived(gather[group].at[unit, 0 : n_rows - 1], g_recv.at[base(group) + unit])

            def span(group):
                lo, hi = spans[group]
                return slice(lo * LANES, hi * LANES)

            def multiply(group, unit, start):
                right = gather[group][unit].reshape(width, gather[group].shape[-1])
                slot = peer(unit)
                for plane in range(2):
                    value = jnp.dot(picks[slot, plane], right, preferred_element_type=F32)
                    if start:
                        acc[plane, :, span(group)] = value
                    else:
                        acc[plane, :, span(group)] += value

            home = unit_of(row)
            named = jnp.full((1, LANES), table[col, row]) - row * row_blocks

            def quad_copy(group, there, piece):
                part, rows = piece
                at = part if there is over else share + part
                slot = slot_of(group, piece)
                if group == last and there is over:
                    slot = jnp.where(is_end, slots + part, slot)
                return remote(
                    q_out[group].at[at, rows], q_in[group].at[row, part, rows],
                    d_send.at[0], q_recv.at[slot], {"prow": there},
                )

            def quad(group, unit):
                right = gather[group][unit].reshape(width, gather[group].shape[-1])
                slot = peer(unit)
                sums = [
                    acc[plane, :, span(group)] + jnp.dot(picks[slot, plane], right, preferred_element_type=F32)
                    for plane in range(2)
                ]
                value = join(*sums)
                product = jnp.dot(z_t[...].reshape(2 * width, width), value.astype(BF16), preferred_element_type=F32)
                turns = [(piece, half) for piece in pieces(group) for half in range(2)]
                if group == last:
                    turns = [(piece, half) for piece in pieces(group) for half in (1, 0)]
                for piece, half in turns:
                    part, rows = piece
                    at = (half * share + part) * LANES
                    upper = product[at + rows.start : at + rows.stop]
                    lower = product[at + band_rows + rows.start : at + band_rows + rows.stop]
                    block = join(upper, lower)
                    q_out[group][half * share + part, rows] = block.astype(BF16)
                    if half:
                        own[group][part, rows] = block
                    if half:

                        @pl.when(is_end)
                        def _():
                            quad_copy(group, mate, piece).start()

                    else:
                        quad_copy(group, over, piece).start()

                acc[0, :, span(group)] = value

            for unit in range(n_cols):
                with scope(f"ready_g0_{unit}"):
                    ready(0, unit)
                if unit == n_cols - 1:
                    with scope("ready_home"):
                        for group in groups[1:]:
                            ready(group, home)
                    for group in groups:
                        turned = gather[group][home].reshape(width, gather[group].shape[-1]).T
                        for tile in range(*spans[group]):
                            at = (tile - spans[group][0]) * LANES
                            to = (tile % share) * LANES
                            part = jnp.where(over - first == tile // share, 0, 1)
                            z_t[part, to : to + LANES, :] = turned[at : at + LANES]
                with scope(f"wpick_{unit}"):
                    if unit > 0:
                        pick_copy(unit, peer(unit)).wait_recv()
                if unit < n_cols - 1:
                    multiply(0, unit, unit == 0)
            with scope("quad0"):
                quad(0, n_cols - 1)
            for group in groups[1:]:
                for i in range(n_cols):
                    unit = (home + i) % n_cols
                    if i > 0:
                        with scope(f"ready_g{group}_{i}"):
                            ready(group, unit)
                    if i < n_cols - 1:
                        multiply(group, unit, i == 0)
                with scope(f"quad{group}"):
                    quad(group, unit)

            for pair in range(width // LANES):
                at = 2 * pair * LANES
                planes = cross(acc[0, :, at : at + LANES], acc[0, :, at + LANES : at + 2 * LANES])
                columns = slice(pair * LANES, (pair + 1) * LANES)
                for i in range(row_blocks):
                    keep = -(named == i).astype(F32)
                    for plane in range(2):
                        sel_out[plane, i * width : (i + 1) * width, columns] = planes[plane] * keep
            copy_k.wait()
            drain(pr.at[0 : n_cols - 1], p_send.at[0])
            drain(pick_out, a_send.at[0])

            @pl.when(is_inner)
            def _():
                drain(picks, g_send.at[0])

            @pl.when(is_end)
            def _():
                drain(picks.at[0:2], g_send.at[0])
                drain(picks.at[0], d_send.at[0])

        pl.run_scoped(
            gathering, dma((4,)), dma((1,)), dma((n_cols - 1,)), dma((1,)), dma((n_cols - 1,)), dma((1,)), dma((4 * n_cols + 1,))
        )

        @pl.when(is_inner)
        def _():
            for group in groups[:last]:
                for piece in pieces(group):
                    part, rows = piece
                    with scope(f"wq{slot_of(group, piece)}"):
                        arrived(q_in[group].at[0 : n_rows - 1, part, rows], q_recv.at[slot_of(group, piece)])
                    total = own[group][part, rows]
                    for source in (over, end, far):
                        total = total + q_in[group][source, part, rows].astype(F32)
                    tot[group][(row - first) * share + part, rows] = total.astype(BF16)
                    total_copy(group, piece, far).start()
                    total_copy(group, piece, end).start()
            for piece in pieces(last):
                part, rows = piece
                slot = slot_of(last, piece)
                with scope(f"wq{slot}"):
                    arrived(q_in[last].at[0:2, part, rows], q_recv.at[slot])
                total = own[last][part] + q_in[last][over, part].astype(F32) + q_in[last][end, part].astype(F32)
                some[part] = total.astype(BF16)
                band = (row - first) * share + part
                remote(
                    some.at[part], tot[last].at[band], d_send.at[0], t_recv.at[2 * last + row - first], {"prow": far}
                ).start()
            for piece in pieces(last):
                part, rows = piece
                with scope(f"wf{part}"):
                    arrived(q_in[last].at[0, part, rows], q_recv.at[slots + part])
                total = some[part].astype(F32) + q_in[last][far, part].astype(F32)
                tot[last][(row - first) * share + part] = total.astype(BF16)
                total_copy(last, piece, end).start()
            for group in groups:
                for part in range(share):
                    total_copy(group, (part, slice(0, band_rows)), over).start()
            for pair in range(width // LANES):
                finish(pair, row - first)

    pl.run_scoped(adding, dma((5 * share,)))

    def total_wait(group, owner):
        arrived(tot[group].at[0:share], t_recv.at[group * 2 + owner])

    @pl.when(is_end)
    def _():
        for group in groups:
            for there in (inner, over):
                with scope(f"wt{group}"):
                    total_wait(group, there - first)
                if group == last and there is over:
                    for part in range(share):
                        band = (over - first) * share + part
                        total = tot[last][band].astype(F32) + q_out[last][part].astype(F32)
                        tot[last][band] = total.astype(BF16)
                if group != 1:
                    finish(1 if group else 0, there - first)

    @pl.when(is_inner)
    def _():
        for group in groups:
            with scope(f"wt{group}"):
                total_wait(group, over - first)
        for pair in range(width // LANES):
            finish(pair, over - first)
        drain(picks.at[0:2], d_send.at[0])


def place(sel, diag, sel_out, diag_out, out_sem):
    copies = [
        pltpu.make_async_copy(sel, sel_out, out_sem.at[0]),
        pltpu.make_async_copy(diag, diag_out, out_sem.at[1]),
    ]
    for copy in copies:
        copy.start()
    for copy in copies:
        copy.wait()


def compact(ainv_anc, panel, u_inv, k_inv, structure):
    n_rows, n_cols = lax.axis_size("prow"), lax.axis_size("pcol")
    width, part = u_inv.shape[-1], panel.shape[2]
    row_blocks = ainv_anc.shape[1] // width
    tiles = 2 * width // LANES
    share = tiles // 2
    spans = ((0, share), (share, share + share // 2), (share + share // 2, tiles))
    hbm = pl.BlockSpec(memory_space=pltpu.HBM)
    vmem = pl.BlockSpec(memory_space=pltpu.VMEM)
    dma = pltpu.SemaphoreType.DMA
    shapes = (
        jax.ShapeDtypeStruct((2, row_blocks * width, width), F32),
        jax.ShapeDtypeStruct(k_inv.shape, F32),
    )

    def per_group(lead, rows, kind):
        return [pltpu.VMEM(lead + (rows, (hi - lo) * LANES), kind) for lo, hi in spans]

    band_rows = LANES // 2
    results = pl.pallas_call(
        functools.partial(kernel, n_rows, n_cols, spans),
        out_shape=tuple(pltpu.VMEM(s.shape, s.dtype) for s in shapes),
        in_specs=[hbm, hbm, hbm, hbm, hbm],
        out_specs=(vmem, vmem),
        scratch_shapes=[
            pltpu.SMEM(structure.shape, jnp.int32),
            pltpu.VMEM(ainv_anc.shape, BF16),
            pltpu.VMEM(panel.shape, BF16),
            pltpu.VMEM((2, width, width), BF16),
            pltpu.VMEM((n_cols, 2, part, width), BF16),
            pltpu.VMEM((n_cols - 1, 2, width, width), BF16),
            pltpu.VMEM((n_cols, 2, width, width), BF16),
            pltpu.VMEM((2, width, 2 * width), F32),
            pltpu.VMEM(k_inv.shape, F32),
            pltpu.VMEM((2, width, width), BF16),
            *per_group((n_cols, n_rows), part, BF16),
            *per_group((share,), band_rows, F32),
            *per_group((tiles,), band_rows, BF16),
            *per_group((n_rows, share), band_rows, BF16),
            *per_group((tiles,), band_rows, BF16),
            pltpu.VMEM((share, band_rows, LANES), BF16),
            dma((1,)),
            dma((6,)),
        ],
        compiler_params=pltpu.CompilerParams(
            collective_id=0, has_side_effects=True
        ),
    )(ainv_anc, panel, u_inv, k_inv, structure)
    return pl.pallas_call(
        place,
        out_shape=shapes,
        in_specs=[vmem, vmem],
        out_specs=(hbm, hbm),
        scratch_shapes=[dma((2,))],
    )(*[pltpu.with_memory_space_constraint(x, pltpu.VMEM) for x in results])


def complex_quad(z_part, s_part):
    highest = lax.Precision.HIGHEST

    def single(left, right):
        return jnp.einsum("kra,rkb->kab", left, right, precision=highest)

    real = single(z_part[0], s_part[0]) - single(z_part[1], s_part[1])
    imag = single(z_part[0], s_part[1]) + single(z_part[1], s_part[0])
    return jnp.stack([real, imag])


def local(ainv_anc, panel, u_inv, k_inv, structure):
    block_width = u_inv.shape[-1]
    cols = lax.axis_size("pcol")
    if (
        structure.shape[1] == cols
        and lax.axis_size("prow") == cols
        and ainv_anc.shape[1] == ainv_anc.shape[2]
        and u_inv.shape[1] == cols
        and cols // 2 == 2
        and cols % 2 == 0
        and block_width == 2 * LANES
    ):
        return compact(ainv_anc, panel, u_inv, k_inv, structure)
    total_k = u_inv.shape[1]
    own_k = k_inv.shape[1]
    n_cols = lax.axis_size("pcol")
    row_here = lax.axis_index("prow")
    col_here = lax.axis_index("pcol")
    row_blocks = ainv_anc.shape[1] // block_width
    group_blocks = ainv_anc.shape[2] // block_width
    group_slots = structure.shape[1] // n_cols
    rows_all = row_blocks * block_width
    col_struct = lax.dynamic_slice_in_dim(structure, col_here * group_slots, group_slots, 1)
    slot_live = col_struct >= 0
    slot_pos = col_struct - col_here * group_blocks
    first_block = row_here * row_blocks
    target = first_block + jnp.arange(row_blocks, dtype=jnp.int32)
    rows_in = lax.all_gather(panel, "prow", axis=2, tiled=True)

    def single(left, right):
        return jnp.einsum("knb,kbc->knc", left, right, preferred_element_type=jnp.float32)

    real = single(rows_in[0], u_inv[0]) - single(rows_in[1], u_inv[1])
    imag = single(rows_in[0], u_inv[1]) + single(rows_in[1], u_inv[0])
    placed = jnp.stack([real, imag]).astype(jnp.bfloat16)
    placed = placed.reshape(2, total_k, group_slots, block_width, block_width)
    placed = jnp.where(slot_live[None, :, :, None, None], placed, jnp.zeros((), jnp.bfloat16))
    block_ids = jnp.arange(group_blocks, dtype=jnp.int32)
    pick_table = (slot_pos[:, :, None] == block_ids[None, None, :]).astype(jnp.bfloat16)
    ainv_blocks = ainv_anc.reshape(2, rows_all, group_blocks, block_width)

    def one_node(items):
        table_k, rows_k = items
        picked = jnp.einsum(
            "sg,cigw->cisw", table_k, ainv_blocks, preferred_element_type=jnp.float32
        )
        picked = picked.astype(jnp.bfloat16).reshape(2, rows_all, group_slots * block_width)
        right = rows_k.reshape(2, group_slots * block_width, block_width)
        real = jnp.dot(picked[0], right[0], preferred_element_type=jnp.float32) - jnp.dot(
            picked[1], right[1], preferred_element_type=jnp.float32
        )
        imag = jnp.dot(picked[0], right[1], preferred_element_type=jnp.float32) + jnp.dot(
            picked[1], right[0], preferred_element_type=jnp.float32
        )
        return jnp.stack([real, imag])

    per_node = lax.map(one_node, (pick_table, jnp.moveaxis(placed, 1, 0)))
    partial_value = jnp.transpose(per_node, (1, 2, 0, 3))
    row_table = (col_struct[:, None, :] == target[None, :, None]).astype(jnp.bfloat16)
    z_rows = jnp.einsum("kts,ckswb->cktwb", row_table, placed, preferred_element_type=jnp.float32)
    z_rows = z_rows.astype(jnp.bfloat16).reshape(2, total_k, rows_all, block_width)
    summed = lax.psum_scatter(
        partial_value.reshape(2, rows_all, total_k * block_width),
        "pcol",
        scatter_dimension=2,
        tiled=True,
    )
    own_struct = lax.dynamic_slice_in_dim(structure, col_here * own_k, own_k, 0)
    member = jnp.any(own_struct[:, :, None] == target[None, None, :], axis=1)
    selected = -summed.reshape(2, row_blocks, block_width, own_k, block_width)
    selected = jnp.where(member.T[None, :, None, :, None], selected, 0.0)
    sel_inv = selected.reshape(2, rows_all, own_k * block_width)
    received = lax.all_to_all(z_rows, "pcol", split_axis=1, concat_axis=1, tiled=True)
    z_own = (
        received.astype(jnp.float32).reshape(2, n_cols, own_k, rows_all, block_width).sum(axis=1)
    )
    quad_term = complex_quad(z_own, selected.reshape(2, rows_all, own_k, block_width))
    total_sum = lax.psum(quad_term, "prow")
    diag_inv = k_inv - total_sum
    return (sel_inv, diag_inv)


def solution(mesh):
    placed = (
        P(None, ("pole", "prow"), "pcol"),
        P(None, "pole", ("pcol", "prow"), None),
        P(None, "pole", None, None),
        P(None, ("pole", "pcol"), None, None),
        P(),
    )
    return jax.shard_map(
        local,
        mesh=mesh,
        in_specs=placed,
        out_specs=(P(None, ("pole", "prow"), "pcol"), P(None, ("pole", "pcol"), None, None)),
        check_vma=False,
    )
```

time: 34.7 us -> 34.4 us (level)
  no operation moved by 1% of the time
where the time goes in v9:
time: 34.4 us; the launch traced here: 34.2 us
  Pallas kernels  33.6 us (98%)
  between operations  0.64 us (2%)
    pallas_call x1, Pallas kernels, compact(): pl.pallas_call(functools.partial(kernel, n_rows, n_cols, spans), out_shap...  32.4 us
    pallas_call x1, Pallas kernels, compact(): pl.pallas_call(place, out_shape=shapes, in_specs=[vmem, vmem], out_specs=...  1.16 us

profile of v9, /device:TPU:0, one launch (start us, length us, event | category | flops | bytes accessed | tf_op | source)
XLA Modules:
  0.0 34.2 jit_solution(7938931945602896871)
XLA Ops:
  0.6 32.4 %shard_map.68 = (f32[2,512,256]{2,1,0:T(8,128)S(1)}, f32[2,1,256,256]{3,2,1,0:T(8,128)S(1)}) custom-call(bf16[2,512,512]{2,1,0:T(8,128)(2,1)} %a_hbm.1, bf16[2,4,64,256]{3,2,1,0:T(8,128)(2,1)} %panel_hbm.1, bf16[2,4,256,256]{3,2,1,0:T(8,128)(2,1)} %u_hbm.1, f32[2,1,256,256]{3,2,1,0:T(8,128)} %k_hbm.1, s32[4,4]{1,0:T(4,128)} %table_hbm.1), custom_call_target="tpu_custom_call" | custom-call | tf_op jit(solution)/shard_map/pallas_call | solution.py:566
  33.1 1.2 %shard_map.69 = (f32[2,512,256]{2,1,0:T(8,128)}, f32[2,1,256,256]{3,2,1,0:T(8,128)}) custom-call(f32[2,512,256]{2,1,0:T(8,128)S(1)} %get-tuple-element.4.sel, f32[2,1,256,256]{3,2,1,0:T(8,128)S(1)} %get-tuple-element.5.diag), custom_call_target="tpu_custom_call" | custom-call | tf_op jit(solution)/shard_map/pallas_call | solution.py:595

commit v10 on v9

--- a/solution.py
+++ b/solution.py
@@ -128,6 +128,17 @@
                 diag_out[plane, 0, rows, columns] = kv[plane, 0, rows, columns] + planes[plane]
 
     dma = pltpu.SemaphoreType.DMA
+
+    def put_sel():
+        named = jnp.full((1, LANES), table[col, row]) - row * row_blocks
+        for pair in range(width // LANES):
+            at = 2 * pair * LANES
+            planes = cross(acc[0, :, at : at + LANES], acc[0, :, at + LANES : at + 2 * LANES])
+            columns = slice(pair * LANES, (pair + 1) * LANES)
+            for i in range(row_blocks):
+                keep = -(named == i).astype(F32)
+                for plane in range(2):
+                    sel_out[plane, i * width : (i + 1) * width, columns] = planes[plane] * keep
 
     def adding(q_recv):
         def gathering(local_sem, p_send, p_recv, a_send, a_recv, g_send, g_recv):
@@ -442,14 +453,10 @@
                 with scope(f"quad{group}"):
                     quad(group, unit)
 
-            for pair in range(width // LANES):
-                at = 2 * pair * LANES
-                planes = cross(acc[0, :, at : at + LANES], acc[0, :, at + LANES : at + 2 * LANES])
-                columns = slice(pair * LANES, (pair + 1) * LANES)
-                for i in range(row_blocks):
-                    keep = -(named == i).astype(F32)
-                    for plane in range(2):
-                        sel_out[plane, i * width : (i + 1) * width, columns] = planes[plane] * keep
+            @pl.when(is_end)
+            def _():
+                put_sel()
+
             copy_k.wait()
             drain(pr.at[0 : n_cols - 1], p_send.at[0])
             drain(pick_out, a_send.at[0])
@@ -501,6 +508,7 @@
             for group in groups:
                 for part in range(share):
                     total_copy(group, (part, slice(0, band_rows)), over).start()
+            put_sel()
             for pair in range(width // LANES):
                 finish(pair, row - first)
 

time: 34.4 us -> 34.4 us (level)
  no operation moved by 1% of the time
where the time goes in v10:
time: 34.4 us; the launch traced here: 34.2 us
  Pallas kernels  33.6 us (98%)
  between operations  0.64 us (2%)
    pallas_call x1, Pallas kernels, compact(): pl.pallas_call(functools.partial(kernel, n_rows, n_cols, spans), out_shap...  32.4 us
    pallas_call x1, Pallas kernels, compact(): pl.pallas_call(place, out_shape=shapes, in_specs=[vmem, vmem], out_specs=...  1.16 us

profile of v10, /device:TPU:0, one launch (start us, length us, event | category | flops | bytes accessed | tf_op | source)
XLA Modules:
  0.0 34.2 jit_solution(2815504888872568906)
XLA Ops:
  0.6 32.4 %shard_map.68 = (f32[2,512,256]{2,1,0:T(8,128)S(1)}, f32[2,1,256,256]{3,2,1,0:T(8,128)S(1)}) custom-call(bf16[2,512,512]{2,1,0:T(8,128)(2,1)} %a_hbm.1, bf16[2,4,64,256]{3,2,1,0:T(8,128)(2,1)} %panel_hbm.1, bf16[2,4,256,256]{3,2,1,0:T(8,128)(2,1)} %u_hbm.1, f32[2,1,256,256]{3,2,1,0:T(8,128)} %k_hbm.1, s32[4,4]{1,0:T(4,128)} %table_hbm.1), custom_call_target="tpu_custom_call" | custom-call | tf_op jit(solution)/shard_map/pallas_call | solution.py:574
  33.1 1.2 %shard_map.69 = (f32[2,512,256]{2,1,0:T(8,128)}, f32[2,1,256,256]{3,2,1,0:T(8,128)}) custom-call(f32[2,512,256]{2,1,0:T(8,128)S(1)} %get-tuple-element.4.sel, f32[2,1,256,256]{3,2,1,0:T(8,128)S(1)} %get-tuple-element.5.diag), custom_call_target="tpu_custom_call" | custom-call | tf_op jit(solution)/shard_map/pallas_call | solution.py:603
